TPU v7x, 128 devices: a whole 4x4x4 slice. The times are simulated.
128 devices in a mesh: var: 16 (over x, y), samp: 8 (over z, core).
Axes of the slice: x: 4, y: 4, z: 4, core: 2. Of those that a mesh axis runs over, the one named last changes fastest.
Arguments:
- dosage: int32 [24576, 8192], P('samp', 'var'), may hold values from 0 to 2, as said below
- phenotype: float32 [24576], P('samp'), may hold values from -6 to 6
- perm_index: int32 [1024, 24576], P('var', 'samp'), may hold values from 0 to 24575, each once within a row
- seg_lengths: int32 [128], replicated, may hold values from 1 to 128, 8192 in all
Outputs:
- zscore: float32 [1024, 8192], P('samp', 'var')
- thresholds: float32 [1024, 128], P('samp')
Inputs may be any that keep to these rules, and one draw needn't show every extreme that they name: `dosage`: each entry is an allele count. `perm_index`: each row is a permutation of the 24576 sample numbers. `seg_lengths`: the lengths sum to 8192, one of them equals 128.
All inputs are finite; a program needn't handle non-finite values.
Results may differ from a plain program's by a relative error of at most 0.0039.
Values may be sent and summed in bfloat16 or wider, within the bound.
A program may use at most 64 MiB of HBM per device.

v0:
```python
import math

import jax
import jax.numpy as jnp
from jax import lax
from jax.sharding import PartitionSpec as P

epsilon = 1e-05


def in_order(blocks, dim):
    blocks = jnp.moveaxis(blocks, 0, dim)
    shape = blocks.shape
    return blocks.reshape(*shape[:dim], shape[dim] * shape[dim + 1], *shape[dim + 2 :])


def sent_to_all(value, axis):
    count = lax.axis_size(axis)
    return lax.all_to_all(
        jnp.broadcast_to(value[None], (count, *value.shape)), axis, 0, 0, tiled=True
    )


def collect(value, axis, dim):
    return in_order(sent_to_all(value, axis), dim)


def taken_together(value, axis):
    return sent_to_all(value, axis).sum(axis=0)


def packed_total(arrays, axis):
    ends = [0]
    for a in arrays:
        ends.append(ends[-1] + a.size)
    subtotal = taken_together(jnp.concatenate([a.ravel() for a in arrays]), axis)
    return tuple((subtotal[b:e].reshape(a.shape) for a, b, e in zip(arrays, ends, ends[1:])))


def cut_along(value, dim, count):
    before, after = (value.shape[:dim], value.shape[dim + 1 :])
    return jnp.moveaxis(value.reshape(*before, count, -1, *after), dim, 0)


def sum_at_owner(value, axis, dim):
    count = lax.axis_size(axis)
    blocks = lax.all_to_all(cut_along(value, dim, count), axis, 0, 0, tiled=True)
    return jnp.sum(blocks, axis=0)


def of_everyone(value, axis):
    return sent_to_all(value, axis).max(axis=0)


def pick_traits(rounded, perm_index):
    count_all = rounded.shape[0]
    low_width = math.gcd(128, count_all)
    high_count = count_all // low_width
    table = rounded.reshape(high_count, low_width)
    flat_index = perm_index.reshape(-1)
    entries = flat_index.shape[0]
    block_size = math.gcd(entries, 16384)
    blocks = flat_index.reshape(entries // block_size, block_size)

    def one_block(index_block):
        high_part = index_block // low_width
        low_part = index_block % low_width
        high_iota = lax.broadcasted_iota(jnp.int32, (block_size, high_count), 1)
        selector = (high_part[:, None] == high_iota).astype(jnp.bfloat16)
        table_rows = jnp.dot(selector, table, preferred_element_type=jnp.float32)
        low_iota = lax.broadcasted_iota(jnp.int32, (block_size, low_width), 1)
        chosen = jnp.sum(jnp.where(low_part[:, None] == low_iota, table_rows, 0.0), axis=1)
        return chosen.astype(jnp.bfloat16)

    picked_all = lax.map(one_block, blocks)
    return picked_all.reshape(perm_index.shape)


def running_max(values):
    width = values.shape[1]
    offset = 1
    while offset < width:
        shifted = jnp.pad(values[:, : width - offset], ((0, 0), (offset, 0)))
        values = jnp.maximum(values, shifted)
        offset = offset * 2
    return values


def per_device(dosage, phenotype, perm_index, seg_lengths):
    pheno_all = collect(phenotype, "samp", 0)
    count_all = pheno_all.shape[0]
    centered = pheno_all - jnp.mean(pheno_all)
    pheno_var = jnp.mean(centered * centered)
    rounded = centered.astype(jnp.bfloat16)
    permuted = pick_traits(rounded, perm_index)
    allele_sum, allele_sq = packed_total(
        (
            jnp.sum(dosage, axis=0).astype(jnp.float32),
            jnp.sum(dosage * dosage, axis=0).astype(jnp.float32),
        ),
        "samp",
    )
    allele_var = allele_sq / count_all - (allele_sum / count_all) ** 2
    dosage_bf = dosage.astype(jnp.bfloat16)
    all_perms = lax.all_gather(permuted, "var", axis=0, tiled=True)
    score = sum_at_owner(
        jnp.dot(all_perms, dosage_bf, preferred_element_type=jnp.float32), "samp", 0
    )
    divisor = jnp.sqrt(count_all * (pheno_var + epsilon) * (allele_var + epsilon))
    zscore = score / divisor[None, :]
    local_prefix = running_max(jnp.abs(zscore))
    block_max = local_prefix[:, -1]
    block_maxima = collect(block_max[None, :], "var", 0)
    position = lax.broadcasted_iota(jnp.int32, block_maxima.shape, 0)
    before = jnp.max(jnp.where(position < lax.axis_index("var"), block_maxima, 0.0), axis=0)
    prefix = jnp.maximum(local_prefix, before[:, None])
    width = dosage.shape[1]
    segment_end = jnp.cumsum(seg_lengths) - 1
    local_end = segment_end - lax.axis_index("var") * width
    column_iota = lax.broadcasted_iota(jnp.int32, (width, local_end.shape[0]), 0)
    match = column_iota == local_end[None, :]
    picked = jnp.max(jnp.where(match[None, :, :], prefix[:, :, None], 0.0), axis=1)
    thresholds = of_everyone(picked, "var")
    return (zscore, thresholds)


def solution(mesh):
    return jax.shard_map(
        per_device,
        mesh=mesh,
        in_specs=(P("samp", "var"), P("samp"), P("var", "samp"), P()),
        out_specs=(P("samp", "var"), P("samp", None)),
        check_vma=False,
    )
```

profile of v0, /device:TPU:0, one launch (start us, length us, event | category | flops | bytes accessed | tf_op | source)
XLA Modules:
  0.0 239.6 jit_solution(4275792382053469606)
XLA Ops:
  7.2 1.4 broadcast_in_dim.69
  8.6 5.4 %all-to-all-start = ((f32[8,1,3072]{2,1,0:T(1,128)}), f32[8,1,3072]{2,1,0:T(1,128)S(1)}, u32[]{:S(2)}, u32[]{:S(2)}) async-start(f32[8,1,3072]{2,1,0:T(1,128)} %broadcast_in_dim.69), calls=%async_computation | async-start | bytes 196608 | tf_op jit(solution)/shard_map/all_to_all | solution.py:19
  14.0 1.5 reshape_reshape.3
  15.5 4.3 %all-to-all-done = f32[8,1,3072]{2,1,0:T(1,128)S(1)} async-done(((f32[8,1,3072]{2,1,0:T(1,128)}), f32[8,1,3072]{2,1,0:T(1,128)S(1)}, u32[]{:S(2)}, u32[]{:S(2)}) %all-to-all-start) | async-done | bytes 98336 | tf_op jit(solution)/shard_map/all_to_all | solution.py:19
  19.8 0.8 reduce_sum.66
  21.2 0.3 convert_reduce_fusion
  21.5 62.9 %while.12 = (s32[]{:T(128)}, bf16[12,16384]{1,0:T(8,128)(2,1)S(1)}, s32[12,16384]{1,0:T(8,128)S(1)}, bf16[192,128]{1,0:T(8,128)(2,1)S(1)}, s32[]{:T(128)}, /*index=5*/s32[]{:T(128)}) while((s32[]{:T(128)}, bf16[12,16384]{1,0:T(8,128)(2,1)S(1)}, s32[12,16384]{1,0:T(8,128)S(1)}, bf16[192,128]{1,0:T(8,128)(2,1)S(1)}, s32[]{:T(128)}, ...), condition=%wide.region_3.4_spmd, body=%wide.region_1.3_spmd.sunk | while | flops 815038464 | bytes 671821 | solution.py:75
  21.7 3.9 %fusion.13 = bf16[16384]{0:T(1024)(128)(2,1)S(1)} fusion(bf16[192,128]{1,0:T(8,128)(2,1)S(1)} %get-tuple-element.117, s32[16384]{0:T(1024)S(1)} %get-tuple-element.100, s32[16384]{0:T(1024)S(1)} %get-tuple-element.101), kind=kOutput, calls=%fused_computation.4.clone.1 | convolution fusion | flops 814727168 | bytes 212992 | tf_op jit(solution)/shard_map/while/body/eval_jaxpr/dot_general | solution.py:70
  25.6 1.1 dynamic_update_slice.8
  26.9 3.9 %fusion.13 = bf16[16384]{0:T(1024)(128)(2,1)S(1)} fusion(bf16[192,128]{1,0:T(8,128)(2,1)S(1)} %get-tuple-element.117, s32[16384]{0:T(1024)S(1)} %get-tuple-element.100, s32[16384]{0:T(1024)S(1)} %get-tuple-element.101), kind=kOutput, calls=%fused_computation.4.clone.1 | convolution fusion | flops 814727168 | bytes 212992 | tf_op jit(solution)/shard_map/while/body/eval_jaxpr/dot_general | solution.py:70
  30.9 1.1 dynamic_update_slice.8
  32.2 3.9 %fusion.13 = bf16[16384]{0:T(1024)(128)(2,1)S(1)} fusion(bf16[192,128]{1,0:T(8,128)(2,1)S(1)} %get-tuple-element.117, s32[16384]{0:T(1024)S(1)} %get-tuple-element.100, s32[16384]{0:T(1024)S(1)} %get-tuple-element.101), kind=kOutput, calls=%fused_computation.4.clone.1 | convolution fusion | flops 814727168 | bytes 212992 | tf_op jit(solution)/shard_map/while/body/eval_jaxpr/dot_general | solution.py:70
  36.1 1.1 dynamic_update_slice.8
  37.4 3.9 %fusion.13 = bf16[16384]{0:T(1024)(128)(2,1)S(1)} fusion(bf16[192,128]{1,0:T(8,128)(2,1)S(1)} %get-tuple-element.117, s32[16384]{0:T(1024)S(1)} %get-tuple-element.100, s32[16384]{0:T(1024)S(1)} %get-tuple-element.101), kind=kOutput, calls=%fused_computation.4.clone.1 | convolution fusion | flops 814727168 | bytes 212992 | tf_op jit(solution)/shard_map/while/body/eval_jaxpr/dot_general | solution.py:70
  41.3 1.1 dynamic_update_slice.8
  42.6 3.9 %fusion.13 = bf16[16384]{0:T(1024)(128)(2,1)S(1)} fusion(bf16[192,128]{1,0:T(8,128)(2,1)S(1)} %get-tuple-element.117, s32[16384]{0:T(1024)S(1)} %get-tuple-element.100, s32[16384]{0:T(1024)S(1)} %get-tuple-element.101), kind=kOutput, calls=%fused_computation.4.clone.1 | convolution fusion | flops 814727168 | bytes 212992 | tf_op jit(solution)/shard_map/while/body/eval_jaxpr/dot_general | solution.py:70
  46.6 1.1 dynamic_update_slice.8
  47.9 3.9 %fusion.13 = bf16[16384]{0:T(1024)(128)(2,1)S(1)} fusion(bf16[192,128]{1,0:T(8,128)(2,1)S(1)} %get-tuple-element.117, s32[16384]{0:T(1024)S(1)} %get-tuple-element.100, s32[16384]{0:T(1024)S(1)} %get-tuple-element.101), kind=kOutput, calls=%fused_computation.4.clone.1 | convolution fusion | flops 814727168 | bytes 212992 | tf_op jit(solution)/shard_map/while/body/eval_jaxpr/dot_general | solution.py:70
  51.8 1.1 dynamic_update_slice.8
  53.1 3.9 %fusion.13 = bf16[16384]{0:T(1024)(128)(2,1)S(1)} fusion(bf16[192,128]{1,0:T(8,128)(2,1)S(1)} %get-tuple-element.117, s32[16384]{0:T(1024)S(1)} %get-tuple-element.100, s32[16384]{0:T(1024)S(1)} %get-tuple-element.101), kind=kOutput, calls=%fused_computation.4.clone.1 | convolution fusion | flops 814727168 | bytes 212992 | tf_op jit(solution)/shard_map/while/body/eval_jaxpr/dot_general | solution.py:70
  57.1 1.1 dynamic_update_slice.8
  58.3 3.9 %fusion.13 = bf16[16384]{0:T(1024)(128)(2,1)S(1)} fusion(bf16[192,128]{1,0:T(8,128)(2,1)S(1)} %get-tuple-element.117, s32[16384]{0:T(1024)S(1)} %get-tuple-element.100, s32[16384]{0:T(1024)S(1)} %get-tuple-element.101), kind=kOutput, calls=%fused_computation.4.clone.1 | convolution fusion | flops 814727168 | bytes 212992 | tf_op jit(solution)/shard_map/while/body/eval_jaxpr/dot_general | solution.py:70
  62.3 1.1 dynamic_update_slice.8
  63.6 3.9 %fusion.13 = bf16[16384]{0:T(1024)(128)(2,1)S(1)} fusion(bf16[192,128]{1,0:T(8,128)(2,1)S(1)} %get-tuple-element.117, s32[16384]{0:T(1024)S(1)} %get-tuple-element.100, s32[16384]{0:T(1024)S(1)} %get-tuple-element.101), kind=kOutput, calls=%fused_computation.4.clone.1 | convolution fusion | flops 814727168 | bytes 212992 | tf_op jit(solution)/shard_map/while/body/eval_jaxpr/dot_general | solution.py:70
  67.5 1.1 dynamic_update_slice.8
  68.8 3.9 %fusion.13 = bf16[16384]{0:T(1024)(128)(2,1)S(1)} fusion(bf16[192,128]{1,0:T(8,128)(2,1)S(1)} %get-tuple-element.117, s32[16384]{0:T(1024)S(1)} %get-tuple-element.100, s32[16384]{0:T(1024)S(1)} %get-tuple-element.101), kind=kOutput, calls=%fused_computation.4.clone.1 | convolution fusion | flops 814727168 | bytes 212992 | tf_op jit(solution)/shard_map/while/body/eval_jaxpr/dot_general | solution.py:70
  72.8 1.1 dynamic_update_slice.8
  74.1 3.9 %fusion.13 = bf16[16384]{0:T(1024)(128)(2,1)S(1)} fusion(bf16[192,128]{1,0:T(8,128)(2,1)S(1)} %get-tuple-element.117, s32[16384]{0:T(1024)S(1)} %get-tuple-element.100, s32[16384]{0:T(1024)S(1)} %get-tuple-element.101), kind=kOutput, calls=%fused_computation.4.clone.1 | convolution fusion | flops 814727168 | bytes 212992 | tf_op jit(solution)/shard_map/while/body/eval_jaxpr/dot_general | solution.py:70
  78.0 1.1 dynamic_update_slice.8
  79.3 3.9 %fusion.13 = bf16[16384]{0:T(1024)(128)(2,1)S(1)} fusion(bf16[192,128]{1,0:T(8,128)(2,1)S(1)} %get-tuple-element.117, s32[16384]{0:T(1024)S(1)} %get-tuple-element.100, s32[16384]{0:T(1024)S(1)} %get-tuple-element.101), kind=kOutput, calls=%fused_computation.4.clone.1 | convolution fusion | flops 814727168 | bytes 212992 | tf_op jit(solution)/shard_map/while/body/eval_jaxpr/dot_general | solution.py:70
  83.2 1.1 dynamic_update_slice.8
  84.4 1.3 reshape.151
  85.8 3.5 %fusion.6 = (s32[512]{0:T(512)S(1)}, s32[512]{0:T(512)S(1)}) fusion(s32[3072,512]{1,0:T(8,128)} %param.6), kind=kLoop, calls=%fused_computation.38 | loop fusion | flops 4717568 | bytes 6295552 | tf_op jit(solution)/shard_map/reduce_sum | solution.py:98
  89.3 0.6 broadcast_in_dim.70
  90.0 3.3 %all-to-all-start.2 = ((f32[8,1,1024]{2,1,0:T(1,128)}), f32[8,1,1024]{2,1,0:T(1,128)S(1)}, u32[]{:S(2)}, u32[]{:S(2)}) async-start(f32[8,1,1024]{2,1,0:T(1,128)} %broadcast_in_dim.70), calls=%async_computation.2 | async-start | bytes 65536 | tf_op jit(solution)/shard_map/all_to_all | solution.py:19
  93.3 53.3 %all-gather.2.cloned.1.call-done = bf16[1024,3072]{1,0:T(8,128)(2,1)} async-done(((bf16[64,3072]{1,0:T(8,128)(2,1)}), bf16[1024,3072]{1,0:T(8,128)(2,1)}) %all-gather.2.cloned.1.call-update) | async-done | bytes 6291472 | tf_op jit(solution)/shard_map/all_gather | solution.py:105
  146.6 9.4 %fusion.4 = f32[1024,512]{1,0:T(8,128)} fusion(bf16[1024,3072]{1,0:T(8,128)(2,1)} %all-gather.2.cloned.1.call-done, s32[3072,512]{1,0:T(8,128)} %param.6), kind=kOutput, calls=%fused_computation.16 | convolution fusion | flops 3222798336 | bytes 14680064 | tf_op jit(solution)/shard_map/dot_general | solution.py:107
  155.9 4.4 %all-to-all-start.1 = ((f32[8,128,512]{2,1,0:T(8,128)}), f32[8,128,512]{2,1,0:T(8,128)S(1)}, u32[]{:S(2)}, u32[]{:S(2)}) async-start(f32[8,128,512]{2,1,0:T(8,128)} %bitcast.24), calls=%async_computation.1 | async-start | bytes 4194304 | tf_op jit(solution)/shard_map/all_to_all | solution.py:47
  160.9 0.8 multiply_reduce_fusion.1
  162.3 25.2 %all-to-all-done.1 = f32[8,128,512]{2,1,0:T(8,128)S(1)} async-done(((f32[8,128,512]{2,1,0:T(8,128)}), f32[8,128,512]{2,1,0:T(8,128)S(1)}, u32[]{:S(2)}, u32[]{:S(2)}) %all-to-all-start.1) | async-done | bytes 2097184 | tf_op jit(solution)/shard_map/all_to_all | solution.py:47
  187.5 0.2 reduce_sum.67
  188.9 0.2 slice_reduce_fusion
  189.1 0.6 broadcast_in_dim.73
  189.7 5.3 %all-to-all-start.3 = ((f32[16,1,128]{2,1,0:T(1,128)}), f32[16,1,128]{2,1,0:T(1,128)S(1)}, u32[]{:S(2)}, u32[]{:S(2)}) async-start(f32[16,1,128]{2,1,0:T(1,128)} %broadcast_in_dim.73), calls=%async_computation.3 | async-start | bytes 16384 | tf_op jit(solution)/shard_map/all_to_all | solution.py:19
  195.0 7.5 %all-to-all-done.3 = f32[16,1,128]{2,1,0:T(1,128)S(1)} async-done(((f32[16,1,128]{2,1,0:T(1,128)}), f32[16,1,128]{2,1,0:T(1,128)S(1)}, u32[]{:S(2)}, u32[]{:S(2)}) %all-to-all-start.3) | async-done | bytes 8224 | tf_op jit(solution)/shard_map/all_to_all | solution.py:19
  202.7 10.9 %select_reduce_fusion = f32[128,128]{1,0:T(8,128)S(1)} fusion(f32[128,512]{1,0:T(8,128)S(1)} %broadcast_maximum_fusion, pred[512,128]{1,0:T(8,128)(4,1)S(1)} %iota_compare_fusion.5), kind=kLoop, calls=%fused_computation.14 | loop fusion | flops 16760832 | bytes 393216 | tf_op jit(solution)/shard_map/reduce_max | solution.py:122
  213.7 18.4 %all_to_all.27 = f32[16,128,128]{2,1,0:T(8,128)S(1)} all-to-all(f32[16,128,128]{2,1,0:T(8,128)S(1)} %broadcast_in_dim.77), channel_id=1, replica_groups=mesh['var'=16,'samp'=8] {'var'}, dimensions={0} | all-to-all | bytes 2097152 | tf_op jit(solution)/shard_map/all_to_all | solution.py:19
  232.1 0.7 reduce_max.29
  (70 shorter events, 3.8 us)
Async XLA Ops:
  8.6 11.2 %all-to-all-start = ((f32[8,1,3072]{2,1,0:T(1,128)}), f32[8,1,3072]{2,1,0:T(1,128)S(1)}, u32[]{:S(2)}, u32[]{:S(2)}) async-start(f32[8,1,3072]{2,1,0:T(1,128)} %broadcast_in_dim.69), calls=%async_computation | async-start | bytes 196608 | tf_op jit(solution)/shard_map/all_to_all | solution.py:19
  14.0 132.6 %all-gather.2.cloned.1.call-start = ((), (), s32[]{:S(2)}) async-start(), calls=%async_computation.5 | async-start | bytes 6684672 | tf_op jit(solution)/shard_map/all_gather | solution.py:105
  90.0 66.0 %all-to-all-start.2 = ((f32[8,1,1024]{2,1,0:T(1,128)}), f32[8,1,1024]{2,1,0:T(1,128)S(1)}, u32[]{:S(2)}, u32[]{:S(2)}) async-start(f32[8,1,1024]{2,1,0:T(1,128)} %broadcast_in_dim.70), calls=%async_computation.2 | async-start | bytes 65536 | tf_op jit(solution)/shard_map/all_to_all | solution.py:19
  93.3 67.1 %copy-start.1 = (s32[128]{0:T(128)S(1)}, s32[128]{0:T(128)}, u32[]{:S(2)}) copy-start(s32[128]{0:T(128)} %param.9) | copy-start | bytes 1540
  155.9 31.6 %all-to-all-start.1 = ((f32[8,128,512]{2,1,0:T(8,128)}), f32[8,128,512]{2,1,0:T(8,128)S(1)}, u32[]{:S(2)}, u32[]{:S(2)}) async-start(f32[8,128,512]{2,1,0:T(8,128)} %bitcast.24), calls=%async_computation.1 | async-start | bytes 4194304 | tf_op jit(solution)/shard_map/all_to_all | solution.py:47
  187.8 45.0 %copy-start = (f32[128,512]{1,0:T(8,128)}, f32[128,512]{1,0:T(8,128)S(1)}, u32[]{:S(2)}) copy-start(f32[128,512]{1,0:T(8,128)S(1)} %get-tuple-element.70) | copy-start | bytes 786436
  189.7 12.8 %all-to-all-start.3 = ((f32[16,1,128]{2,1,0:T(1,128)}), f32[16,1,128]{2,1,0:T(1,128)S(1)}, u32[]{:S(2)}, u32[]{:S(2)}) async-start(f32[16,1,128]{2,1,0:T(1,128)} %broadcast_in_dim.73), calls=%async_computation.3 | async-start | bytes 16384 | tf_op jit(solution)/shard_map/all_to_all | solution.py:19
Sparse Core Ops, SparseCore 0:
  85.9 60.6 all-gather.1
where the time goes:
time: 240 us
  waiting for transfers between devices  90.2 us (38%)
  matrix products  56.2 us (23%)
  local copies, waits for them, and re-layouts  20.6 us (9%)
  other arithmetic  19.6 us (8%)
  starting transfers between devices  18.5 us (8%)
  blocking collectives  18.4 us (8%)
  between operations  15.6 us (6%)
    all_gather x1, waiting for transfers between devices, per_device(): all_perms = lax.all_gather(permuted, 'var', axis=0, tiled=True)  53.3 us
    dot_general x12, matrix products, one_block(): table_rows = jnp.dot(selector, table, preferred_element_type=jnp.float32)  46.8 us
    all_to_all x1, waiting for transfers between devices, sum_at_owner(): lax.all_to_all(cut_along(value, dim, count), axis, 0, 0, tiled=True)  25.2 us
    all_to_all x1, blocking collectives, sent_to_all(): lax.all_to_all(jnp.broadcast_to(value[None], (count, *value.shape)), axis...  18.4 us
    all_to_all x3, starting transfers between devices, sent_to_all(): lax.all_to_all(jnp.broadcast_to(value[None], (count, *value.shape)), axis...  14 us
    dynamic_update_slice x12, local copies, waits for them, and re-layouts, pick_traits(): picked_all = lax.map(one_block, blocks)  13.7 us
    all_to_all x3, waiting for transfers between devices, sent_to_all(): lax.all_to_all(jnp.broadcast_to(value[None], (count, *value.shape)), axis...  11.8 us
    reduce_max x1, other arithmetic, per_device(): jnp.max(jnp.where(match[None, :, :], prefix[:, :, None], 0.0), axis=1)  10.9 us
  transfers between devices with their start and end apart: 5, of which 4 were waited for; matrix products, arithmetic and copies ran while one was open for 7% of the time, Pallas kernels for 0%

commit v1 on v0

v1 whole, which is shorter than its diff:
```python
import jax
import jax.numpy as jnp
from jax import lax
from jax.experimental import pallas as pl
from jax.experimental.pallas import tpu as pltpu
from jax.sharding import PartitionSpec as P

epsilon = 1e-05
top = 32767.0


def in_order(blocks, dim):
    blocks = jnp.moveaxis(blocks, 0, dim)
    shape = blocks.shape
    return blocks.reshape(*shape[:dim], shape[dim] * shape[dim + 1], *shape[dim + 2 :])


def sent_to_all(value, axis):
    count = lax.axis_size(axis)
    return lax.all_to_all(
        jnp.broadcast_to(value[None], (count, *value.shape)), axis, 0, 0, tiled=True
    )


def collect(value, axis, dim):
    return in_order(sent_to_all(value, axis), dim)


def cut_along(value, dim, count):
    before, after = (value.shape[:dim], value.shape[dim + 1 :])
    return jnp.moveaxis(value.reshape(*before, count, -1, *after), dim, 0)


def sum_at_owner(value, axis, dim):
    count = lax.axis_size(axis)
    blocks = lax.all_to_all(cut_along(value, dim, count), axis, 0, 0, tiled=True)
    return jnp.sum(blocks, axis=0)


def looked_up(index, table_ref, half_at):
    high_half = index >= half_at
    word = jnp.where(high_half, index - half_at, index)
    lane = lax.bitwise_and(word, 127)
    row = lax.shift_right_logical(word, 7)
    rows = half_at // 128
    levels = max(1, (rows - 1).bit_length())
    bits = [lax.bitwise_and(row, 1 << k) != 0 for k in range(levels)]

    def pick(level, base):
        if level == 0:
            source = table_ref[pl.ds(base * 8, 8), :]
            return jnp.take_along_axis(source, lane, axis=1, mode="promise_in_bounds")
        low = pick(level - 1, base)
        if base + (1 << (level - 1)) >= rows:
            return low
        high = pick(level - 1, base + (1 << (level - 1)))
        return jnp.where(bits[level - 1], high, low)

    words = pick(levels, 0)
    low_part = lax.shift_right_arithmetic(lax.shift_left(words, 16), 16)
    return jnp.where(high_half, lax.shift_right_arithmetic(words, 16), low_part)


def gather_kernel(index_ref, table_ref, scale_ref, out_ref):
    rows, width = index_ref.shape
    half_at = table_ref.shape[0] // 8 * 128
    scale = scale_ref[0]

    @pl.loop(0, rows // 16)
    def _(r):
        @pl.loop(0, width // 128)
        def _(j):
            columns = pl.ds(pl.multiple_of(j * 128, 128), 128)
            parts = []
            for h in range(2):
                at = pl.ds(pl.multiple_of(r * 16 + 8 * h, 8), 8)
                picked = looked_up(index_ref[at, columns], table_ref, half_at)
                parts.append(picked.astype(jnp.float32) * scale)
            both = jnp.concatenate(parts, axis=0).astype(jnp.bfloat16)
            out_ref[pl.ds(pl.multiple_of(r * 16, 16), 16), columns] = both


def pick_traits(centered, perm_index):
    count_all = centered.shape[0]
    largest = jnp.max(jnp.abs(centered))
    unit = jnp.where(largest > 0, largest / top, 1.0)
    fixed = jnp.round(centered / unit).astype(jnp.int32)
    half = count_all // 2
    words = jnp.bitwise_or(jnp.bitwise_and(fixed[:half], 65535), fixed[half:] << 16)
    table = jnp.repeat(words.reshape(half // 128, 128), 8, axis=0)
    return pl.pallas_call(
        gather_kernel,
        out_shape=jax.ShapeDtypeStruct(perm_index.shape, jnp.bfloat16),
        in_specs=[
            pl.BlockSpec(memory_space=pltpu.VMEM),
            pl.BlockSpec(memory_space=pltpu.VMEM),
            pl.BlockSpec(memory_space=pltpu.SMEM),
        ],
        out_specs=pl.BlockSpec(memory_space=pltpu.VMEM),
    )(perm_index, table, unit.reshape(1))


def running_max(values):
    width = values.shape[1]
    offset = 1
    while offset < width:
        shifted = jnp.pad(values[:, : width - offset], ((0, 0), (offset, 0)))
        values = jnp.maximum(values, shifted)
        offset = offset * 2
    return values


def per_device(dosage, phenotype, perm_index, seg_lengths):
    pheno_all = collect(phenotype, "samp", 0)
    count_all = pheno_all.shape[0]
    centered = pheno_all - jnp.mean(pheno_all)
    pheno_var = jnp.mean(centered * centered)
    permuted = pick_traits(centered, perm_index)
    counts = jnp.stack([jnp.sum(dosage, axis=0), jnp.sum(dosage * dosage, axis=0)])
    counts = sent_to_all(counts.astype(jnp.float32), "samp").sum(axis=0)
    allele_var = counts[1] / count_all - (counts[0] / count_all) ** 2
    dosage_bf = dosage.astype(jnp.bfloat16)
    all_perms = lax.all_gather(permuted, "var", axis=0, tiled=True)
    score = sum_at_owner(
        jnp.dot(all_perms, dosage_bf, preferred_element_type=jnp.float32), "samp", 0
    )
    divisor = jnp.sqrt(count_all * (pheno_var + epsilon) * (allele_var + epsilon))
    zscore = score / divisor[None, :]
    local_prefix = running_max(jnp.abs(zscore))
    width = dosage.shape[1]
    segment_end = jnp.cumsum(seg_lengths) - 1
    local_end = jnp.minimum(segment_end - lax.axis_index("var") * width, width - 1)
    column_iota = lax.broadcasted_iota(jnp.int32, (width, local_end.shape[0]), 0)
    match = column_iota == local_end[None, :]
    picked = jnp.max(jnp.where(match[None, :, :], local_prefix[:, :, None], 0.0), axis=1)
    count = lax.axis_size("var")
    mine = lax.all_to_all(cut_along(picked, 0, count), "var", 0, 0, tiled=True).max(axis=0)
    thresholds = collect(mine, "var", 0)
    return (zscore, thresholds)


def solution(mesh):
    return jax.shard_map(
        per_device,
        mesh=mesh,
        in_specs=(P("samp", "var"), P("samp"), P("var", "samp"), P()),
        out_specs=(P("samp", "var"), P("samp", None)),
        check_vma=False,
    )
```

time: 240 us -> 199 us (0.83)
  matrix products: 56.2 us -> 9.36 us
  Pallas kernels: 0 us -> 30.1 us
  local copies, waits for them, and re-layouts: 20.6 us -> 2.94 us
  blocking collectives: 18.4 us -> 34.6 us
  waiting for transfers between devices: 90.2 us -> 79.3 us
  starting transfers between devices: 18.5 us -> 7.81 us
    dot_general x12 -> x0, matrix products: 46.8 us -> none  [one_block(): table_rows = jnp.dot(selector, table, preferred_element_type=jnp.float32)]
    pallas_call x0 -> x1, Pallas kernels: none -> 30.1 us  [pick_traits(): pl.pallas_call(gather_kernel, out_shape=jax.ShapeDtypeStruct(perm_index.s...]
    dynamic_update_slice x12 -> x0, local copies, waits for them, and re-layouts: 13.7 us -> none  [pick_traits(): picked_all = lax.map(one_block, blocks)]
    all_to_all x0 -> x1, blocking collectives: none -> 12.7 us  [per_device(): lax.all_to_all(cut_along(picked, 0, count), 'var', 0, 0, tiled=True)]
    all_to_all x3 -> x1, waiting for transfers between devices: 11.8 us -> 0.01 us  [sent_to_all(): lax.all_to_all(jnp.broadcast_to(value[None], (count, *value.shape)), axis...]
    all_to_all x3 -> x1, starting transfers between devices: 14 us -> 3.34 us  [sent_to_all(): lax.all_to_all(jnp.broadcast_to(value[None], (count, *value.shape)), axis...]
    all_to_all x1 -> x2, blocking collectives: 18.4 us -> 21.9 us  [sent_to_all(): lax.all_to_all(jnp.broadcast_to(value[None], (count, *value.shape)), axis...]
    reduce_max x3 -> x2, other arithmetic: 11.7 us -> 11 us  [the longest x1 11 us: per_device(): jnp.max(jnp.where(match[None, :, :], local_prefix[:, :, None], 0.0), axis=1)]
  transfers between devices with their start and end apart: 5 -> 3, of which waited for: 4 -> 2; matrix products, arithmetic and copies ran while one was open for 7% -> 7% of each run, Pallas kernels for 0% -> 0%
where the time goes in v1:
time: 199 us
  waiting for transfers between devices  79.3 us (40%)
  blocking collectives  34.6 us (17%)
  Pallas kernels  30.1 us (15%)
  other arithmetic  18.1 us (9%)
  between operations  16.8 us (8%)
  matrix products  9.36 us (5%)
  starting transfers between devices  7.81 us (4%)
  local copies, waits for them, and re-layouts  2.94 us (1%)
    all_gather x1, waiting for transfers between devices, per_device(): all_perms = lax.all_gather(permuted, 'var', axis=0, tiled=True)  53.3 us
    pallas_call x1, Pallas kernels, pick_traits(): pl.pallas_call(gather_kernel, out_shape=jax.ShapeDtypeStruct(perm_index.s...  30.1 us
    all_to_all x1, waiting for transfers between devices, sum_at_owner(): lax.all_to_all(cut_along(value, dim, count), axis, 0, 0, tiled=True)  26 us
    all_to_all x2, blocking collectives, sent_to_all(): lax.all_to_all(jnp.broadcast_to(value[None], (count, *value.shape)), axis...  21.9 us
    all_to_all x1, blocking collectives, per_device(): lax.all_to_all(cut_along(picked, 0, count), 'var', 0, 0, tiled=True)  12.7 us
    reduce_max x1, other arithmetic, per_device(): jnp.max(jnp.where(match[None, :, :], local_prefix[:, :, None], 0.0), axis=1)  11 us
    dot_general x1, matrix products, per_device(): jnp.dot(all_perms, dosage_bf, preferred_element_type=jnp.float32)  9.36 us
    all_to_all x1, starting transfers between devices, sum_at_owner(): lax.all_to_all(cut_along(value, dim, count), axis, 0, 0, tiled=True)  4.43 us
  transfers between devices with their start and end apart: 3, of which 2 were waited for; matrix products, arithmetic and copies ran while one was open for 7% of the time, Pallas kernels for 0%

profile of v1, /device:TPU:0, one launch (start us, length us, event | category | flops | bytes accessed | tf_op | source)
XLA Modules:
  0.0 198.9 jit_solution(11497866706915802541)
XLA Ops:
  7.2 0.0 all-gather.2.cloned.1.call-start
  7.2 0.8 broadcast_in_dim.28
  8.0 11.0 %all_to_all.26 = f32[8,1,3072]{2,1,0:T(1,128)S(1)} all-to-all(f32[8,1,3072]{2,1,0:T(1,128)S(1)} %broadcast_in_dim.28), channel_id=1, replica_groups=mesh['var'=16,'samp'=8] {'samp'}, dimensions={0} | all-to-all | bytes 196608 | tf_op jit(solution)/shard_map/all_to_all | solution.py:20
  19.0 0.8 reduce_sum.54
  20.4 0.9 multiply_reduce_fusion.1
  22.6 0.1 round-nearest-even_convert_fusion
  22.7 0.1 fusion.2
  22.8 0.8 broadcast_bitcast_fusion.table_ref
  23.5 30.1 %shard_map.59 = bf16[64,3072]{1,0:T(8,128)(2,1)} custom-call(s32[64,3072]{1,0:T(8,128)} %index_ref.1, s32[768,128]{1,0:T(8,128)} %broadcast_bitcast_fusion.table_ref, f32[1]{0:T(128)} %bitcast.2.scale_ref), custom_call_target="tpu_custom_call" | custom-call | tf_op jit(solution)/shard_map/pallas_call | solution.py:91
  53.6 0.0 all-gather.2.cloned.1.call-update
  53.6 3.5 %fusion.5 = (s32[512]{0:T(512)S(1)}, s32[512]{0:T(512)S(1)}) fusion(s32[3072,512]{1,0:T(8,128)} %param.4), kind=kLoop, calls=%fused_computation.30 | loop fusion | flops 4717568 | bytes 6295552 | tf_op jit(solution)/shard_map/reduce_sum | solution.py:119
  57.2 0.6 broadcast_in_dim.30
  57.8 3.3 %all-to-all-start.2 = ((f32[8,2,512]{2,1,0:T(2,128)}), f32[8,2,512]{2,1,0:T(2,128)S(1)}, u32[]{:S(2)}, u32[]{:S(2)}) async-start(f32[8,2,512]{2,1,0:T(2,128)} %broadcast_in_dim.30), calls=%async_computation.2 | async-start | bytes 65536 | tf_op jit(solution)/shard_map/all_to_all | solution.py:20
  61.2 0.0 copy-start.1
  61.2 53.3 %all-gather.2.cloned.1.call-done = bf16[1024,3072]{1,0:T(8,128)(2,1)} async-done(((bf16[64,3072]{1,0:T(8,128)(2,1)}), bf16[1024,3072]{1,0:T(8,128)(2,1)}) %all-gather.2.cloned.1.call-update) | async-done | bytes 6291472 | tf_op jit(solution)/shard_map/all_gather | solution.py:123
  114.4 9.4 %fusion = f32[1024,512]{1,0:T(8,128)} fusion(bf16[1024,3072]{1,0:T(8,128)(2,1)} %all-gather.2.cloned.1.call-done, s32[3072,512]{1,0:T(8,128)} %param.4), kind=kOutput, calls=%fused_computation.2 | convolution fusion | flops 3222798336 | bytes 14680064 | tf_op jit(solution)/shard_map/dot_general | solution.py:125
  123.8 0.0 all-to-all-done.2
  123.8 4.4 %all-to-all-start.1 = ((f32[8,128,512]{2,1,0:T(8,128)}), f32[8,128,512]{2,1,0:T(8,128)S(1)}, u32[]{:S(2)}, u32[]{:S(2)}) async-start(f32[8,128,512]{2,1,0:T(8,128)} %bitcast.25), calls=%async_computation.1 | async-start | bytes 4194304 | tf_op jit(solution)/shard_map/all_to_all | solution.py:36
  128.2 0.0 copy-done.1
  128.2 0.1 copy.11
  128.4 0.2 reduce-window.8
  128.5 0.1 minimum_reduce_fusion
  128.6 0.1 iota_compare_fusion
  129.4 26.0 %all-to-all-done.1 = f32[8,128,512]{2,1,0:T(8,128)S(1)} async-done(((f32[8,128,512]{2,1,0:T(8,128)}), f32[8,128,512]{2,1,0:T(8,128)S(1)}, u32[]{:S(2)}, u32[]{:S(2)}) %all-to-all-start.1) | async-done | bytes 2097184 | tf_op jit(solution)/shard_map/all_to_all | solution.py:36
  155.4 0.2 reduce_sum.55
  155.7 0.0 copy-start
  155.7 0.1 pad_maximum_fusion.8
  155.8 0.1 pad_maximum_fusion.7
  156.0 0.1 pad_maximum_fusion.6
  156.1 0.1 pad_maximum_fusion.5
  156.3 0.1 pad_maximum_fusion.4
  156.4 0.1 pad_maximum_fusion.3
  156.6 0.1 pad_maximum_fusion.2
  156.8 11.0 %select_reduce_fusion = f32[128,128]{1,0:T(8,128)S(1)} fusion(f32[128,512]{1,0:T(8,128)S(1)} %pad_maximum_fusion, pred[512,128]{1,0:T(8,128)(4,1)S(1)} %iota_compare_fusion), kind=kLoop, calls=%fused_computation | loop fusion | flops 16760832 | bytes 393216 | tf_op jit(solution)/shard_map/reduce_max | solution.py:135
  167.8 12.7 %all_to_all.27 = f32[16,8,128]{2,1,0:T(8,128)S(1)} all-to-all(f32[16,8,128]{2,1,0:T(8,128)S(1)} %bitcast.28), channel_id=1, replica_groups=mesh['var'=16,'samp'=8] {'var'}, dimensions={0} | all-to-all | bytes 131072 | tf_op jit(solution)/shard_map/all_to_all | solution.py:137
  180.6 10.9 %all_to_all.28 = f32[16,8,128]{2,1,0:T(8,128)S(1)} all-to-all(f32[16,8,128]{2,1,0:T(8,128)S(1)} %broadcast_in_dim.51), channel_id=1, replica_groups=mesh['var'=16,'samp'=8] {'var'}, dimensions={0} | all-to-all | bytes 131072 | tf_op jit(solution)/shard_map/all_to_all | solution.py:20
  191.5 0.6 copy.16
  192.1 0.0 copy-done
  (10 shorter events, 0.2 us)
Async XLA Ops:
  7.2 107.3 %all-gather.2.cloned.1.call-start = ((), (), s32[]{:S(2)}) async-start(), calls=%async_computation.5 | async-start | bytes 6684672 | tf_op jit(solution)/shard_map/all_gather | solution.py:123
  57.8 66.0 %all-to-all-start.2 = ((f32[8,2,512]{2,1,0:T(2,128)}), f32[8,2,512]{2,1,0:T(2,128)S(1)}, u32[]{:S(2)}, u32[]{:S(2)}) async-start(f32[8,2,512]{2,1,0:T(2,128)} %broadcast_in_dim.30), calls=%async_computation.2 | async-start | bytes 65536 | tf_op jit(solution)/shard_map/all_to_all | solution.py:20
  61.2 67.1 %copy-start.1 = (s32[128]{0:T(128)S(1)}, s32[128]{0:T(128)}, u32[]{:S(2)}) copy-start(s32[128]{0:T(128)} %param.7) | copy-start | bytes 1540
  123.8 31.6 %all-to-all-start.1 = ((f32[8,128,512]{2,1,0:T(8,128)}), f32[8,128,512]{2,1,0:T(8,128)S(1)}, u32[]{:S(2)}, u32[]{:S(2)}) async-start(f32[8,128,512]{2,1,0:T(8,128)} %bitcast.25), calls=%async_computation.1 | async-start | bytes 4194304 | tf_op jit(solution)/shard_map/all_to_all | solution.py:36
  155.7 36.4 %copy-start = (f32[128,512]{1,0:T(8,128)}, f32[128,512]{1,0:T(8,128)S(1)}, u32[]{:S(2)}) copy-start(f32[128,512]{1,0:T(8,128)S(1)} %get-tuple-element.10) | copy-start | bytes 786436
Sparse Core Ops, SparseCore 0:
  53.8 60.6 all-gather.1

commit v2 on v1

v2 whole, which is shorter than its diff:
```python
import jax
import jax.numpy as jnp
from jax import lax
from jax.experimental import pallas as pl
from jax.experimental.pallas import tpu as pltpu
from jax.sharding import PartitionSpec as P

epsilon = 1e-05
top = 32767.0
side = 4
chunks = 4
rows = 16
parts = 4
pieces = 4
MESH = pl.DeviceIdType.MESH


def looked_up(index, table_ref, half_at):
    high_half = index >= half_at
    word = jnp.where(high_half, index - half_at, index)
    lane = lax.bitwise_and(word, 127)
    row = lax.shift_right_logical(word, 7)
    count = half_at // 128
    levels = max(1, (count - 1).bit_length())
    bits = [lax.bitwise_and(row, 1 << k) != 0 for k in range(levels)]

    def pick(level, base):
        if level == 0:
            source = table_ref[pl.ds(base * 8, 8), :]
            return jnp.take_along_axis(source, lane, axis=1, mode="promise_in_bounds")
        low = pick(level - 1, base)
        if base + (1 << (level - 1)) >= count:
            return low
        high = pick(level - 1, base + (1 << (level - 1)))
        return jnp.where(bits[level - 1], high, low)

    words = pick(levels, 0)
    low_part = lax.shift_right_arithmetic(lax.shift_left(words, 16), 16)
    return jnp.where(high_half, lax.shift_right_arithmetic(words, 16), low_part)


def aligned(value, by):
    return pl.multiple_of(value, by)


def kernel(
    dosage_ref, pheno_ref, index_ref, seg_ref, zscore_ref, thresholds_ref,
    traits, words, table, index, counts, dose, permuted, score, arrived, stats, marks,
    best, best_x, best_xy, best_y,
    local_sem, barrier_pad, trait_send, trait_recv, stat_send, stat_recv, dose_send, dose_recv,
    pass_send, pass_recv, perm_send, perm_recv, score_send, score_recv,
    x_send, x_recv, y_send, y_recv,
):
    samples, width = dosage_ref.shape
    var, samp = lax.axis_index("var"), lax.axis_index("samp")
    x, y = var // side, var % side
    z, core = samp // 2, samp % 2
    all_samples = 8 * samples
    part = 2 * samples // parts
    is_source = y // 2 == core
    own_slot = x * 2 + y % 2
    write_slot = jnp.where(is_source, own_slot, 8)

    def at(dx=0, dy=0):
        return lax.rem(x + dx + side, side) * side + lax.rem(y + dy + side, side)

    def remote(src, dst, send, recv, to_var=None, to_samp=None):
        return pltpu.make_async_remote_copy(
            src_ref=src, dst_ref=dst, send_sem=send, recv_sem=recv,
            device_id={
                "var": var if to_var is None else to_var,
                "samp": samp if to_samp is None else to_samp,
            },
            device_id_type=MESH,
        )

    piece = samples // pieces
    read_pheno = pltpu.make_async_copy(pheno_ref, traits.at[samp], local_sem.at[0])
    read_index = pltpu.make_async_copy(index_ref, index, local_sem.at[1])
    read_seg = pltpu.make_async_copy(seg_ref, marks, local_sem.at[2])
    read_dose = [
        pltpu.make_async_copy(
            dosage_ref.at[pl.ds(i * piece, piece)], counts.at[pl.ds(i * piece, piece)],
            local_sem.at[3 + i],
        )
        for i in range(pieces)
    ]
    read_pheno.start()
    for copy in read_dose[:2]:
        copy.start()
    read_index.start()
    read_seg.start()
    for copy in read_dose[2:]:
        copy.start()

    barrier = pltpu.get_barrier_semaphore()
    samp_peers = [lax.rem(samp + d, 8) for d in range(1, 8)]
    for peer in samp_peers:
        pl.semaphore_signal(barrier, inc=1, device_id={"var": var, "samp": peer}, device_id_type=MESH)
    for d in range(1, side):
        for to in (at(dx=d), at(dy=d)):
            pl.semaphore_signal(barrier, inc=1, device_id={"var": to, "samp": samp}, device_id_type=MESH)
    read_pheno.wait()
    pl.semaphore_wait(barrier, 13)

    trait_copies = [
        remote(traits.at[samp], traits.at[samp], trait_send.at[d], trait_recv.at[d], to_samp=samp_peers[d])
        for d in range(7)
    ]
    for copy in trait_copies:
        copy.start()

    def dose_copy(i):
        at_rows = pl.ds(aligned(core * samples + i * piece, 16), piece)
        return remote(dose.at[at_rows], dose.at[at_rows], dose_send.at[i], dose_recv.at[i], to_samp=samp ^ 1)

    def convert(i):
        read_dose[i].wait()
        step = 32

        def body(r, sums):
            one, two = sums
            for h in range(step // 16):
                start = i * piece + r * step + 16 * h
                value = counts[pl.ds(aligned(start, 16), 16), :].astype(jnp.float32)
                dose[pl.ds(aligned(core * samples + start, 16), 16), :] = value.astype(jnp.bfloat16)
                one = one + (value[:8] + value[8:])
                two = two + (value[:8] * value[:8] + value[8:] * value[8:])
            return one, two

        zero = jnp.zeros((8, width), jnp.float32)
        one, two = lax.fori_loop(0, piece // step, body, (zero, zero))
        if i == 0:
            stats[samp] = jnp.zeros((8, width), jnp.float32)
        stats[samp, 0:1, :] += jnp.sum(one, axis=0, keepdims=True)
        stats[samp, 1:2, :] += jnp.sum(two, axis=0, keepdims=True)
        dose_copy(i).start()

    stat_copies = [
        remote(stats.at[samp], stats.at[samp], stat_send.at[d], stat_recv.at[d], to_samp=samp_peers[d])
        for d in range(7)
    ]

    convert(0)
    convert(1)

    for copy in trait_copies:
        copy.wait_recv()
    high = all_samples // 2 // 128

    values = traits[...].reshape(2 * high, 128)
    mean = jnp.sum(jnp.sum(values, axis=0, keepdims=True), axis=1, keepdims=True) / all_samples
    centered = values - mean
    square = jnp.sum(centered * centered, axis=0, keepdims=True)
    pheno_var = jnp.sum(square, axis=1, keepdims=True) / all_samples
    largest = jnp.max(jnp.max(jnp.abs(centered), axis=0, keepdims=True), axis=1, keepdims=True)
    unit = jnp.where(largest > 0, largest / top, 1.0)
    fixed = jnp.round(centered / unit).astype(jnp.int32)
    words[...] = jnp.bitwise_or(
        jnp.bitwise_and(fixed[:high], 65535), lax.shift_left(fixed[high:], 16)
    )
    for r in range(high):
        table[pl.ds(8 * r, 8), :] = jnp.broadcast_to(words[pl.ds(r, 1), :], (8, 128))
    scale = jnp.broadcast_to(unit, (8, 128))
    read_index.wait()

    def gather(k, half):
        tiles = samples // 128 // 2

        @pl.loop(0, tiles)
        def _(j):
            start = (half * tiles + j) * 128
            both = []
            for h in range(2):
                block = index[pl.ds(k * rows + 8 * h, 8), pl.ds(aligned(start, 128), 128)]
                both.append(looked_up(block, table, high * 128).astype(jnp.float32) * scale)
            permuted[k, write_slot, :, pl.ds(aligned(core * samples + start, 128), 128)] = (
                jnp.concatenate(both, axis=0).astype(jnp.bfloat16)
            )

    def lanes(q):
        return pl.ds(aligned(q * part, 128), part)

    def passed(k, half, from_core):
        q = 2 * from_core + half
        return remote(
            permuted.at[k, 8, :, lanes(q)], permuted.at[k, own_slot, :, lanes(q)],
            pass_send.at[k, half], pass_recv.at[k, half], to_samp=samp ^ 1,
        )

    def pass_on(k, half):
        @pl.when(jnp.logical_not(is_source))
        def _():
            passed(k, half, core).start()

    def moved(axis, by):
        return at(dx=by) if axis == 0 else at(dy=by)

    def sends(k, q, event, slot, directions):
        return [
            remote(
                permuted.at[k, slot, :, lanes(q)], permuted.at[k, slot, :, lanes(q)],
                perm_send.at[k, q, event + i], perm_recv.at[k, q, slot], to_var=moved(axis, by),
            )
            for i, (axis, by) in enumerate(directions)
        ]

    def recv(k, q, slot):
        remote(
            permuted.at[k, slot, :, lanes(q)], permuted.at[k, slot, :, lanes(q)],
            perm_send.at[k, q, 0], perm_recv.at[k, q, slot],
        ).wait_recv()

    def slot_of(dx, dy):
        sx, sy = lax.rem(x - dx + side, side), lax.rem(y - dy + side, side)
        return sx * 2 + lax.rem(sy, 2), sy // 2 == core

    def routes(q):
        return q % 2, (1 if q < 2 else -1)

    def stage(k, q, level, act):
        axis, way = routes(q)
        other = 1 - axis
        if level == 0:
            todo = [(0, 0, 0, [(axis, way), (axis, -way), (other, way), (other, -way)])]
        elif level == 1:
            todo = []
            event = 4
            for d in (way % side, -way % side, 2):
                ways = [(other, way), (other, -way)]
                if d == way % side:
                    ways = [(axis, way), *ways]
                todo.append(((d, 0) if axis == 0 else (0, d), event, ways))
                event += len(ways)
            todo = [(*where, event, ways) for where, event, ways in todo]
        elif level == 2:
            todo = []
            for i, d in enumerate((0, way % side, -way % side, 2)):
                where = (d, way % side) if axis == 0 else (way % side, d)
                todo.append((*where, 11 + i, [(other, way)]))
        else:
            todo = []
            for far in (-way % side, 2):
                for d in range(side):
                    todo.append((*((d, far) if axis == 0 else (far, d)), 0, []))
        for dy in dict.fromkeys(t[1] for t in todo):

            @pl.when(slot_of(0, dy)[1])
            def _(dy=dy):
                for tx, ty, event, ways in todo:
                    if ty == dy:
                        act(k, q, level, slot_of(tx, ty)[0], event, ways)

    def go(k, q, level, slot, event, ways):
        if level:
            recv(k, q, slot)
        for copy in sends(k, q, event, slot, ways):
            copy.start()

    def done(k, q, level, slot, event, ways):
        for copy in sends(k, q, event, slot, ways):
            copy.wait_send()

    def stages(k, level, act=go):
        for q in range(parts):
            stage(k, q, level, act)

    def send_own(k, half):
        for q in range(parts):
            if q % 2 == half:

                @pl.when(jnp.logical_and(is_source, q // 2 == core))
                def _(q=q):
                    stage(k, q, 0, go)

    def send_passed(k, half):
        @pl.when(is_source)
        def _():
            passed(k, half, 1 - core).wait_recv()

        for q in range(parts):
            if q % 2 == half:

                @pl.when(jnp.logical_and(is_source, q // 2 != core))
                def _(q=q):
                    stage(k, q, 0, go)

    def multiply(k):
        @pl.loop(0, parts)
        def _(q):
            left = permuted[k, pl.ds(0, 8), :, lanes(q)].reshape(8 * rows, part)
            product = jnp.dot(
                left, dose[pl.ds(aligned(q * part, 16), part), :], preferred_element_type=jnp.float32
            )

            @pl.when(q == 0)
            def _():
                score[k] = product

            @pl.when(q > 0)
            def _():
                score[k] += product

    def score_copies(k):
        copies = []
        for d in (1, 3, 2):
            to = lax.rem(z + d, side)
            copies.append(
                remote(
                    score.at[k, pl.ds(aligned(to * 2 * rows, 2 * rows), 2 * rows)],
                    arrived.at[k, d - 1], score_send.at[k, d - 1], score_recv.at[k, d - 1],
                    to_samp=to * 2 + core,
                )
            )
        return copies

    def inverse_divisor():
        for copy in stat_copies:
            copy.wait_recv()
        sums = jnp.sum(stats[...], axis=0)
        allele_sum, allele_sq = sums[0:1], sums[1:2]
        allele_var = allele_sq / all_samples - (allele_sum / all_samples) ** 2
        return 1.0 / jnp.sqrt(all_samples * (pheno_var + epsilon) * (allele_var + epsilon))

    lane = lax.broadcasted_iota(jnp.int32, (2 * rows, 128), 1)

    def local_ends():
        ends = jnp.broadcast_to(marks[...], (8, 128))
        lane8 = lax.broadcasted_iota(jnp.int32, (8, 128), 1)
        offset = 1
        while offset < 128:
            ends = ends + jnp.where(lane8 >= offset, pltpu.roll(ends, offset, axis=1), 0)
            offset *= 2
        return ends - 1 - var * width

    def finish(k, inverse, ends):
        for copy in score_copies(k):
            copy.wait_recv()
        total = score[k, pl.ds(aligned(z * 2 * rows, 2 * rows), 2 * rows), :]
        for d in range(3):
            total = total + arrived[k, d]
        result = total * inverse
        zscore_ref[pl.ds(rows * k, rows), :] = result[:rows]
        zscore_ref[pl.ds(64 + rows * k, rows), :] = result[rows:]
        size = jnp.abs(result)
        best_here = jnp.zeros((2 * rows, 128), jnp.float32)
        for t in range(width // 128):
            run = size[:, 128 * t : 128 * (t + 1)]
            offset = 1
            while offset < 128:
                run = jnp.maximum(run, jnp.where(lane >= offset, pltpu.roll(run, offset, axis=1), 0.0))
                offset *= 2
            here = ends - 128 * t
            source = jnp.minimum(jnp.maximum(here, 0), 127)
            found = jnp.concatenate(
                [
                    jnp.where(
                        here >= 0,
                        jnp.take_along_axis(run[8 * g : 8 * g + 8], source, axis=1, mode="promise_in_bounds"),
                        0.0,
                    )
                    for g in range(2 * rows // 8)
                ],
                axis=0,
            )
            best_here = jnp.maximum(best_here, found)
        best[k] = best_here

    def best_copies(k, axis):
        source, target = (best, best_x) if axis == 0 else (best_xy, best_y)
        send, recv_sem = (x_send, x_recv) if axis == 0 else (y_send, y_recv)
        return [
            remote(source.at[k], target.at[k, d - 1], send.at[k, d - 1], recv_sem.at[k, d - 1], to_var=moved(axis, d))
            for d in (1, 3, 2)
        ]

    def join_x(k):
        for copy in best_copies(k, 0):
            copy.wait_recv()
        value = best[k]
        for d in range(3):
            value = jnp.maximum(value, best_x[k, d])
        best_xy[k] = value

    def join_y(k):
        for copy in best_copies(k, 1):
            copy.wait_recv()
        value = best_xy[k]
        for d in range(3):
            value = jnp.maximum(value, best_y[k, d])
        thresholds_ref[pl.ds(rows * k, rows), :] = value[:rows]
        thresholds_ref[pl.ds(64 + rows * k, rows), :] = value[rows:]

    def start(copies):
        for copy in copies:
            copy.start()

    for half in range(2):
        gather(0, half)
        pass_on(0, half)
        send_own(0, half)
    for half in range(2):
        send_passed(0, half)
    convert(2)
    convert(3)
    start(stat_copies)
    stages(0, 1)
    for k in range(1, chunks):
        gather(k, 0)
        pass_on(k, 0)
        send_own(k, 0)
        stages(k - 1, 2)
        gather(k, 1)
        pass_on(k, 1)
        send_own(k, 1)
        for half in range(2):
            send_passed(k, half)
        stages(k, 1)
        stages(k - 1, 3)
        if k == 1:
            for i in range(pieces):
                dose_other = pl.ds(aligned((1 - core) * samples + i * piece, 16), piece)
                remote(dose.at[dose_other], dose.at[dose_other], dose_send.at[i], dose_recv.at[i]).wait_recv()
            read_seg.wait()
        multiply(k - 1)
        start(score_copies(k - 1))
        if k == 2:
            inverse = inverse_divisor()
            ends = local_ends()
        if k >= 2:
            finish(k - 2, inverse, ends)
    last = chunks - 1
    stages(last, 2)
    stages(last, 3)
    multiply(last)
    start(score_copies(last))
    finish(last - 1, inverse, ends)
    for k in range(last):
        start(best_copies(k, 0))
    for k in range(last):
        join_x(k)
        start(best_copies(k, 1))
    finish(last, inverse, ends)
    start(best_copies(last, 0))
    for k in range(last):
        join_y(k)
    for copy in trait_copies + stat_copies + [dose_copy(i) for i in range(pieces)]:
        copy.wait_send()
    for k in range(chunks):
        for level in range(3):
            if level == 0:

                @pl.when(is_source)
                def _(k=k):
                    stages(k, 0, done)

                @pl.when(jnp.logical_not(is_source))
                def _(k=k):
                    for half in range(2):
                        passed(k, half, core).wait_send()

            else:
                stages(k, level, done)
        for copy in score_copies(k):
            copy.wait_send()
    join_x(last)
    start(best_copies(last, 1))
    join_y(last)
    for k in range(chunks):
        for copy in best_copies(k, 0) + best_copies(k, 1):
            copy.wait_send()


def per_device(dosage, phenotype, perm_index, seg_lengths):
    samples, width = dosage.shape
    segments = seg_lengths.shape[0]
    dma = pltpu.SemaphoreType.DMA
    f32, i32, bf16 = jnp.float32, jnp.int32, jnp.bfloat16
    vmem = pltpu.VMEM
    any_space = pl.BlockSpec(memory_space=pl.ANY)
    return pl.pallas_call(
        kernel,
        out_shape=(
            jax.ShapeDtypeStruct((128, width), f32),
            jax.ShapeDtypeStruct((128, segments), f32),
        ),
        in_specs=[any_space] * 4,
        out_specs=(pl.BlockSpec(memory_space=vmem), pl.BlockSpec(memory_space=vmem)),
        scratch_shapes=[
            vmem((8, samples // 128, 128), f32),
            vmem((samples * 4 // 128, 128), i32),
            vmem((samples * 4 // 16, 128), i32),
            vmem(perm_index.shape, i32),
            vmem((samples, width), i32),
            vmem((2 * samples, width), bf16),
            vmem((chunks, 9, rows, 2 * samples), bf16),
            vmem((chunks, 8 * rows, width), f32),
            vmem((chunks, 3, 2 * rows, width), f32),
            vmem((8, 8, width), f32),
            vmem((1, segments), i32),
            vmem((chunks, 2 * rows, segments), f32),
            vmem((chunks, 3, 2 * rows, segments), f32),
            vmem((chunks, 2 * rows, segments), f32),
            vmem((chunks, 3, 2 * rows, segments), f32),
            dma((3 + pieces,)),
            dma((1,)),
            dma((7,)),
            dma((7,)),
            dma((7,)),
            dma((7,)),
            dma((pieces,)),
            dma((pieces,)),
            dma((chunks, 2)),
            dma((chunks, 2)),
            dma((chunks, parts, 15)),
            dma((chunks, parts, 8)),
            dma((chunks, 3)),
            dma((chunks, 3)),
            dma((chunks, 3)),
            dma((chunks, 3)),
            dma((chunks, 3)),
            dma((chunks, 3)),
        ],
        compiler_params=pltpu.CompilerParams(
            collective_id=0, has_side_effects=True, vmem_limit_bytes=60 * 1024 * 1024
        ),
    )(
        dosage,
        phenotype.reshape(samples // 128, 128),
        perm_index,
        seg_lengths.reshape(1, segments),
    )


def solution(mesh):
    return jax.shard_map(
        per_device,
        mesh=mesh,
        in_specs=(P("samp", "var"), P("samp"), P("var", "samp"), P()),
        out_specs=(P("samp", "var"), P("samp", None)),
        check_vma=False,
    )
```

time: 199 us -> 121 us (0.61)
  Pallas kernels: 30.1 us -> 118 us
  waiting for transfers between devices: 79.3 us -> 0 us
  blocking collectives: 34.6 us -> 0 us
  other arithmetic: 18.1 us -> 0 us
  between operations: 16.8 us -> 0.64 us
  matrix products: 9.36 us -> 0 us
  starting transfers between devices: 7.81 us -> 0 us
    pallas_call x1, Pallas kernels: 30.1 us -> 118 us  [per_device(): pl.pallas_call(kernel, out_shape=(jax.ShapeDtypeStruct((128, width), f32)...]
    all_gather x1 -> x0, waiting for transfers between devices: 53.3 us -> none  [per_device(): all_perms = lax.all_gather(permuted, 'var', axis=0, tiled=True)]
    all_to_all x3 -> x0, blocking collectives: 34.6 us -> none  [the longest x2 21.9 us: sent_to_all(): lax.all_to_all(jnp.broadcast_to(value[None], (count, *value.shape)), axis...]
    all_to_all x2 -> x0, waiting for transfers between devices: 26 us -> none  [the longest x1 26 us: sum_at_owner(): lax.all_to_all(cut_along(value, dim, count), axis, 0, 0, tiled=True)]
    reduce_max x2 -> x0, other arithmetic: 11 us -> none  [the longest x1 11 us: per_device(): jnp.max(jnp.where(match[None, :, :], local_prefix[:, :, None], 0.0), axis=1)]
    dot_general x1 -> x0, matrix products: 9.36 us -> none  [per_device(): jnp.dot(all_perms, dosage_bf, preferred_element_type=jnp.float32)]
    all_to_all x2 -> x0, starting transfers between devices: 7.77 us -> none  [the longest x1 4.43 us: sum_at_owner(): lax.all_to_all(cut_along(value, dim, count), axis, 0, 0, tiled=True)]
    reduce_sum x5 -> x0, other arithmetic: 5.42 us -> none  [the longest x1 3.52 us: per_device(): jnp.sum(dosage, axis=0)]
  transfers between devices with their start and end apart: 3 -> 0, of which waited for: 2 -> 0; matrix products, arithmetic and copies ran while one was open for 7% -> 0% of each run, Pallas kernels for 0% -> 0%
where the time goes in v2:
time: 121 us
  Pallas kernels  118 us (98%)
  local copies, waits for them, and re-layouts  3.14 us (3%)
    pallas_call x1, Pallas kernels, per_device(): pl.pallas_call(kernel, out_shape=(jax.ShapeDtypeStruct((128, width), f32)...  118 us
    unnamed x2, local copies, waits for them, and re-layouts  3.14 us

profile of v2, /device:TPU:0, one launch (start us, length us, event | category | flops | bytes accessed | tf_op | source)
XLA Modules:
  0.0 121.3 jit_solution(891173244853106265)
XLA Ops:
  0.6 117.5 %shard_map.59 = (f32[128,512]{1,0:T(8,128)}, f32[128,128]{1,0:T(8,128)}) custom-call(s32[3072,512]{1,0:T(8,128)} %dosage_ref.1, f32[24,128]{1,0:T(8,128)} %bitcast.2, s32[64,3072]{1,0:T(8,128)} %index_ref.1, s32[1,128]{1,0:T(1,128)} %bitcast.3), custom_call_target="tpu_custom_call" | custom-call | tf_op jit(solution)/shard_map/pallas_call | solution.py:481
  118.2 1.7 %copy.8 = f32[128,512]{1,0:T(8,128)} copy(f32[128,512]{1,0:T(8,128)} %get-tuple-element.4) | data formatting | bytes 524288
  119.8 1.5 %copy.9 = f32[128,128]{1,0:T(8,128)} copy(f32[128,128]{1,0:T(8,128)} %get-tuple-element.5) | data formatting | bytes 131072

commit v3 on v2

--- a/solution.py
+++ b/solution.py
@@ -12,7 +12,34 @@
 rows = 16
 parts = 4
 pieces = 4
+group = 2
 MESH = pl.DeviceIdType.MESH
+
+order = [
+    ("gather", 0), ("gather", 1), ("gather", 2), ("own", 0, 0), ("gather", 3), ("gather", 4),
+    ("passed", 0, 0), ("gather", 5), ("own", 0, 1), ("gather", 6), ("ring", 0, 0), ("passed", 0, 1),
+    ("gather", 7), ("gather", 8), ("own", 1, 0), ("ring", 0, 2), ("gather", 9), ("ring", 0, 1),
+    ("passed", 1, 0), ("gather", 10), ("far", 0, 0), ("gather", 11), ("own", 1, 1), ("passed", 1, 1),
+    ("ring", 1, 0), ("side", 0, 0), ("ring", 0, 3), ("far", 0, 2), ("gather", 12), ("gather", 13),
+    ("ring", 1, 2), ("gather", 14), ("own", 2, 0), ("far", 0, 1), ("passed", 2, 0), ("gather", 15),
+    ("side", 0, 2), ("far", 1, 0), ("side", 0, 3), ("ring", 1, 3), ("gather", 16), ("ring", 1, 1),
+    ("far", 1, 2), ("gather", 17), ("own", 2, 1), ("side", 0, 1), ("far", 0, 3), ("side", 1, 0),
+    ("passed", 2, 1), ("gather", 18), ("ring", 2, 2), ("gather", 19), ("ring", 2, 0), ("gather", 20),
+    ("own", 3, 0), ("side", 1, 3), ("passed", 3, 0), ("corner", 0, 1), ("gather", 21), ("side", 1, 2),
+    ("far", 1, 1), ("corner", 0, 3), ("gather", 22), ("ring", 2, 1), ("side", 1, 1), ("corner", 0, 0),
+    ("corner", 1, 0), ("far", 1, 3), ("ring", 2, 3), ("corner", 0, 2), ("gather", 23), ("own", 3, 1),
+    ("corner", 1, 1), ("far", 2, 0), ("passed", 3, 1), ("ring", 3, 0), ("ring", 3, 2), ("far", 2, 1),
+    ("corner", 1, 3), ("far", 2, 3), ("ring", 3, 1), ("corner", 1, 2), ("end", 0, 0), ("far", 2, 2),
+    ("side", 2, 0), ("side", 2, 1), ("end", 0, 1), ("ring", 3, 3), ("corner", 2, 0), ("side", 2, 2),
+    ("multiply", 0, 0), ("multiply", 0, 1), ("side", 2, 3), ("end", 1, 0), ("end", 1, 1), ("far", 3, 2),
+    ("corner", 2, 2), ("far", 3, 1), ("corner", 2, 1), ("far", 3, 0), ("far", 3, 3), ("corner", 2, 3),
+    ("side", 3, 2), ("side", 3, 0), ("multiply", 1, 0), ("multiply", 1, 1), ("finish", 0), ("side", 3, 1),
+    ("side", 3, 3), ("corner", 3, 2), ("corner", 3, 0), ("end", 2, 0), ("multiply", 2, 0), ("corner", 3, 3),
+    ("corner", 3, 1), ("end", 2, 1), ("multiply", 2, 1), ("finish", 1), ("end", 3, 0), ("multiply", 3, 0),
+    ("end", 3, 1), ("multiply", 3, 1), ("finish", 2),
+]
+straight_ring = ()
+straight_side = ()
 
 
 def looked_up(index, table_ref, half_at):
@@ -47,7 +74,7 @@
     dosage_ref, pheno_ref, index_ref, seg_ref, zscore_ref, thresholds_ref,
     traits, words, table, index, counts, dose, permuted, score, arrived, stats, marks,
     best, best_x, best_xy, best_y,
-    local_sem, barrier_pad, trait_send, trait_recv, stat_send, stat_recv, dose_send, dose_recv,
+    local_sem, trait_send, trait_recv, stat_send, stat_recv, dose_send, dose_recv,
     pass_send, pass_recv, perm_send, perm_recv, score_send, score_recv,
     x_send, x_recv, y_send, y_recv,
 ):
@@ -100,15 +127,10 @@
     for d in range(1, side):
         for to in (at(dx=d), at(dy=d)):
             pl.semaphore_signal(barrier, inc=1, device_id={"var": to, "samp": samp}, device_id_type=MESH)
-    read_pheno.wait()
-    pl.semaphore_wait(barrier, 13)
-
     trait_copies = [
         remote(traits.at[samp], traits.at[samp], trait_send.at[d], trait_recv.at[d], to_samp=samp_peers[d])
         for d in range(7)
     ]
-    for copy in trait_copies:
-        copy.start()
 
     def dose_copy(i):
         at_rows = pl.ds(aligned(core * samples + i * piece, 16), piece)
@@ -134,15 +156,18 @@
             stats[samp] = jnp.zeros((8, width), jnp.float32)
         stats[samp, 0:1, :] += jnp.sum(one, axis=0, keepdims=True)
         stats[samp, 1:2, :] += jnp.sum(two, axis=0, keepdims=True)
-        dose_copy(i).start()
 
     stat_copies = [
         remote(stats.at[samp], stats.at[samp], stat_send.at[d], stat_recv.at[d], to_samp=samp_peers[d])
         for d in range(7)
     ]
 
-    convert(0)
-    convert(1)
+    for i in range(pieces):
+        convert(i)
+    read_pheno.wait()
+    pl.semaphore_wait(barrier, 13)
+    for copy in trait_copies:
+        copy.start()
 
     for copy in trait_copies:
         copy.wait_recv()
@@ -164,19 +189,20 @@
     scale = jnp.broadcast_to(unit, (8, 128))
     read_index.wait()
 
-    def gather(k, half):
-        tiles = samples // 128 // 2
-
-        @pl.loop(0, tiles)
+    def gather(i):
+        k, first = i // 6, i % 6 * (samples // 128 // 6)
+
+        @pl.loop(0, samples // 128 // 6 // group)
         def _(j):
-            start = (half * tiles + j) * 128
-            both = []
-            for h in range(2):
-                block = index[pl.ds(k * rows + 8 * h, 8), pl.ds(aligned(start, 128), 128)]
-                both.append(looked_up(block, table, high * 128).astype(jnp.float32) * scale)
-            permuted[k, write_slot, :, pl.ds(aligned(core * samples + start, 128), 128)] = (
-                jnp.concatenate(both, axis=0).astype(jnp.bfloat16)
-            )
+            for t in range(group):
+                start = (first + j * group + t) * 128
+                both = []
+                for h in range(2):
+                    block = index[pl.ds(k * rows + 8 * h, 8), pl.ds(aligned(start, 128), 128)]
+                    both.append(looked_up(block, table, high * 128).astype(jnp.float32) * scale)
+                permuted[k, write_slot, :, pl.ds(aligned(core * samples + start, 128), 128)] = (
+                    jnp.concatenate(both, axis=0).astype(jnp.bfloat16)
+                )
 
     def lanes(q):
         return pl.ds(aligned(q * part, 128), part)
@@ -218,31 +244,35 @@
     def routes(q):
         return q % 2, (1 if q < 2 else -1)
 
-    def stage(k, q, level, act):
+    def cells(k, q, level):
         axis, way = routes(q)
         other = 1 - axis
-        if level == 0:
-            todo = [(0, 0, 0, [(axis, way), (axis, -way), (other, way), (other, -way)])]
-        elif level == 1:
-            todo = []
-            event = 4
-            for d in (way % side, -way % side, 2):
-                ways = [(other, way), (other, -way)]
-                if d == way % side:
-                    ways = [(axis, way), *ways]
-                todo.append(((d, 0) if axis == 0 else (0, d), event, ways))
-                event += len(ways)
-            todo = [(*where, event, ways) for where, event, ways in todo]
-        elif level == 2:
-            todo = []
-            for i, d in enumerate((0, way % side, -way % side, 2)):
-                where = (d, way % side) if axis == 0 else (way % side, d)
-                todo.append((*where, 11 + i, [(other, way)]))
+        unit_no = 2 * k + q % 2
+        straight = unit_no in straight_ring
+        both = [(other, way), (other, -way)]
+        if unit_no in straight_side:
+            both.append((other, 2 * way))
+        near, back = way % side, -way % side
+        if level == "own":
+            ring = [(axis, way), (axis, -way)] + [(axis, 2 * way)] * straight
+            found = [(0, 0, 0, ring + both)]
+        elif level == "ring":
+            found = [(near, 0, 6, [(axis, way)] * (not straight) + both), (back, 0, 10, both)]
+        elif level == "far":
+            found = [(2, 0, 13, both)]
+        elif unit_no in straight_side:
+            ends = level == "end"
+            found = [(d, s, 0, []) for s in (near, back, 2) for d in range(side) if ends]
+        elif level == "side":
+            found = [(d, near, 16 + i, [(other, way)]) for i, d in enumerate((0, near, back))]
+        elif level == "corner":
+            found = [(2, near, 19, [(other, way)])]
         else:
-            todo = []
-            for far in (-way % side, 2):
-                for d in range(side):
-                    todo.append((*((d, far) if axis == 0 else (far, d)), 0, []))
+            found = [(d, s, 0, []) for s in (back, 2) for d in range(side)]
+        return [(p, s, *rest) if axis == 0 else (s, p, *rest) for p, s, *rest in found]
+
+    def stage(k, q, level, act):
+        todo = cells(k, q, level)
         for dy in dict.fromkeys(t[1] for t in todo):
 
             @pl.when(slot_of(0, dy)[1])
@@ -252,7 +282,7 @@
                         act(k, q, level, slot_of(tx, ty)[0], event, ways)
 
     def go(k, q, level, slot, event, ways):
-        if level:
+        if level != "own":
             recv(k, q, slot)
         for copy in sends(k, q, event, slot, ways):
             copy.start()
@@ -261,17 +291,13 @@
         for copy in sends(k, q, event, slot, ways):
             copy.wait_send()
 
-    def stages(k, level, act=go):
-        for q in range(parts):
-            stage(k, q, level, act)
-
     def send_own(k, half):
         for q in range(parts):
             if q % 2 == half:
 
                 @pl.when(jnp.logical_and(is_source, q // 2 == core))
                 def _(q=q):
-                    stage(k, q, 0, go)
+                    stage(k, q, "own", go)
 
     def send_passed(k, half):
         @pl.when(is_source)
@@ -283,23 +309,27 @@
 
                 @pl.when(jnp.logical_and(is_source, q // 2 != core))
                 def _(q=q):
-                    stage(k, q, 0, go)
-
-    def multiply(k):
-        @pl.loop(0, parts)
-        def _(q):
+                    stage(k, q, "own", go)
+
+    def multiply(k, half):
+        @pl.loop(0, parts // 2)
+        def _(i):
+            q = 2 * i + half
             left = permuted[k, pl.ds(0, 8), :, lanes(q)].reshape(8 * rows, part)
             product = jnp.dot(
                 left, dose[pl.ds(aligned(q * part, 16), part), :], preferred_element_type=jnp.float32
             )
-
-            @pl.when(q == 0)
-            def _():
-                score[k] = product
-
-            @pl.when(q > 0)
-            def _():
+            if half:
                 score[k] += product
+            else:
+
+                @pl.when(i == 0)
+                def _():
+                    score[k] = product
+
+                @pl.when(i > 0)
+                def _():
+                    score[k] += product
 
     def score_copies(k):
         copies = []
@@ -395,80 +425,96 @@
         for copy in copies:
             copy.start()
 
-    for half in range(2):
-        gather(0, half)
-        pass_on(0, half)
-        send_own(0, half)
-    for half in range(2):
-        send_passed(0, half)
-    convert(2)
-    convert(3)
-    start(stat_copies)
-    stages(0, 1)
-    for k in range(1, chunks):
-        gather(k, 0)
-        pass_on(k, 0)
-        send_own(k, 0)
-        stages(k - 1, 2)
-        gather(k, 1)
-        pass_on(k, 1)
-        send_own(k, 1)
-        for half in range(2):
-            send_passed(k, half)
-        stages(k, 1)
-        stages(k - 1, 3)
-        if k == 1:
-            for i in range(pieces):
-                dose_other = pl.ds(aligned((1 - core) * samples + i * piece, 16), piece)
-                remote(dose.at[dose_other], dose.at[dose_other], dose_send.at[i], dose_recv.at[i]).wait_recv()
-            read_seg.wait()
-        multiply(k - 1)
-        start(score_copies(k - 1))
-        if k == 2:
-            inverse = inverse_divisor()
-            ends = local_ends()
-        if k >= 2:
-            finish(k - 2, inverse, ends)
+    def wait_dose():
+        for i in range(pieces):
+            theirs = pl.ds(aligned((1 - core) * samples + i * piece, 16), piece)
+            remote(dose.at[theirs], dose.at[theirs], dose_send.at[i], dose_recv.at[i]).wait_recv()
+
+    def drain_passed(k):
+        @pl.when(jnp.logical_not(is_source))
+        def _():
+            for half in range(2):
+                passed(k, half, core).wait_send()
+
     last = chunks - 1
-    stages(last, 2)
-    stages(last, 3)
-    multiply(last)
-    start(score_copies(last))
-    finish(last - 1, inverse, ends)
-    for k in range(last):
-        start(best_copies(k, 0))
-    for k in range(last):
+    sent, finished, started = False, [], []
+    last_send = [e for e in order if e[0] in ("ring", "far", "side", "corner")][-1]
+    for name, *where in order:
+        if name == "gather":
+            gather(*where)
+            if where[0] == 0:
+                start([dose_copy(i) for i in range(pieces)] + stat_copies)
+            if where[0] == 3:
+                read_seg.wait()
+                ends = local_ends()
+        elif name == "own":
+            pass_on(*where)
+            send_own(*where)
+        elif name == "passed":
+            send_passed(*where)
+        elif name == "end":
+            k, half = where
+            for q in range(half, parts, 2):
+                stage(k, q, "end", go)
+        elif name == "multiply":
+            k, half = where
+            if k == 0 and half == 0:
+                wait_dose()
+                inverse = inverse_divisor()
+            multiply(k, half)
+            if half:
+                start(score_copies(k))
+        elif name == "finish":
+            finish(*where, inverse, ends)
+            finished.extend(where)
+        else:
+            stage(*where, name, go)
+        if (name, *where) == last_send:
+            sent = True
+        while sent and len(started) < len(finished):
+            started.append(finished[len(started)])
+            start(best_copies(started[-1], 0))
+    for k in range(last - 1):
         join_x(k)
         start(best_copies(k, 1))
     finish(last, inverse, ends)
     start(best_copies(last, 0))
-    for k in range(last):
-        join_y(k)
+    join_x(last - 1)
+    start(best_copies(last - 1, 1))
     for copy in trait_copies + stat_copies + [dose_copy(i) for i in range(pieces)]:
         copy.wait_send()
     for k in range(chunks):
-        for level in range(3):
-            if level == 0:
-
-                @pl.when(is_source)
-                def _(k=k):
-                    stages(k, 0, done)
-
-                @pl.when(jnp.logical_not(is_source))
-                def _(k=k):
-                    for half in range(2):
-                        passed(k, half, core).wait_send()
-
-            else:
-                stages(k, level, done)
+        drain_passed(k)
+        for q in range(parts):
+            for level in ("own", "ring", "far", "side", "corner"):
+                stage(k, q, level, done)
         for copy in score_copies(k):
             copy.wait_send()
     join_x(last)
     start(best_copies(last, 1))
-    join_y(last)
+    for k in range(chunks):
+        join_y(k)
     for k in range(chunks):
         for copy in best_copies(k, 0) + best_copies(k, 1):
             copy.wait_send()
+
+
+def keep_kernel(zscore_ref, thresholds_ref, zscore_out, thresholds_out, first, second, sem):
+    into = [
+        pltpu.make_async_copy(zscore_ref, first, sem.at[0]),
+        pltpu.make_async_copy(thresholds_ref, second, sem.at[1]),
+    ]
+    out = [
+        pltpu.make_async_copy(first, zscore_out, sem.at[2]),
+        pltpu.make_async_copy(second, thresholds_out, sem.at[3]),
+    ]
+    for copy in into:
+        copy.start()
+    for copy, after in zip(into, out):
+        copy.wait()
+        after.start()
+    for copy in out:
+        copy.wait()
 
 
 def per_device(dosage, phenotype, perm_index, seg_lengths):
@@ -477,13 +523,14 @@
     dma = pltpu.SemaphoreType.DMA
     f32, i32, bf16 = jnp.float32, jnp.int32, jnp.bfloat16
     vmem = pltpu.VMEM
-    any_space = pl.BlockSpec(memory_space=pl.ANY)
-    return pl.pallas_call(
+    any_space = pl.BlockSpec(memory_space=pltpu.HBM)
+    outs = (
+        jax.ShapeDtypeStruct((128, width), f32),
+        jax.ShapeDtypeStruct((128, segments), f32),
+    )
+    zscore, thresholds = pl.pallas_call(
         kernel,
-        out_shape=(
-            jax.ShapeDtypeStruct((128, width), f32),
-            jax.ShapeDtypeStruct((128, segments), f32),
-        ),
+        out_shape=outs,
         in_specs=[any_space] * 4,
         out_specs=(pl.BlockSpec(memory_space=vmem), pl.BlockSpec(memory_space=vmem)),
         scratch_shapes=[
@@ -503,7 +550,6 @@
             vmem((chunks, 2 * rows, segments), f32),
             vmem((chunks, 3, 2 * rows, segments), f32),
             dma((3 + pieces,)),
-            dma((1,)),
             dma((7,)),
             dma((7,)),
             dma((7,)),
@@ -512,7 +558,7 @@
             dma((pieces,)),
             dma((chunks, 2)),
             dma((chunks, 2)),
-            dma((chunks, parts, 15)),
+            dma((chunks, parts, 20)),
             dma((chunks, parts, 8)),
             dma((chunks, 3)),
             dma((chunks, 3)),
@@ -530,6 +576,14 @@
         perm_index,
         seg_lengths.reshape(1, segments),
     )
+    return pl.pallas_call(
+        keep_kernel,
+        out_shape=outs,
+        in_specs=[any_space] * 2,
+        out_specs=(any_space, any_space),
+        scratch_shapes=[vmem((128, width), f32), vmem((128, segments), f32), dma((4,))],
+        compiler_params=pltpu.CompilerParams(vmem_limit_bytes=60 * 1024 * 1024),
+    )(zscore, thresholds)
 
 
 def solution(mesh):

time: 121 us -> 83.8 us (0.69)
  Pallas kernels: 118 us -> 82.8 us
  local copies, waits for them, and re-layouts: 3.14 us -> 0 us
    pallas_call x1 -> x2, Pallas kernels: 118 us -> 82.8 us  [the longest x1 81.1 us: per_device(): pl.pallas_call(kernel, out_shape=outs, in_specs=[any_space] * 4, out_spec...]
    unnamed x2 -> x0, local copies, waits for them, and re-layouts: 3.14 us -> none
where the time goes in v3:
time: 83.8 us; the launch traced here: 83.6 us
  Pallas kernels  82.8 us (99%)
    pallas_call x1, Pallas kernels, per_device(): pl.pallas_call(kernel, out_shape=outs, in_specs=[any_space] * 4, out_spec...  81.1 us
    pallas_call x1, Pallas kernels, per_device(): pl.pallas_call(keep_kernel, out_shape=outs, in_specs=[any_space] * 2, out...  1.7 us

profile of v3, /device:TPU:0, one launch (start us, length us, event | category | flops | bytes accessed | tf_op | source)
XLA Modules:
  0.0 83.6 jit_solution(498748916627761829)
XLA Ops:
  0.6 81.1 %shard_map.59 = (f32[128,512]{1,0:T(8,128)}, f32[128,128]{1,0:T(8,128)}) custom-call(s32[3072,512]{1,0:T(8,128)} %dosage_ref.1, f32[24,128]{1,0:T(8,128)} %bitcast.2, s32[64,3072]{1,0:T(8,128)} %index_ref.1, s32[1,128]{1,0:T(1,128)} %bitcast.3), custom_call_target="tpu_custom_call" | custom-call | tf_op jit(solution)/shard_map/pallas_call | solution.py:531
  81.8 1.7 %shard_map.60 = (f32[128,512]{1,0:T(8,128)}, f32[128,128]{1,0:T(8,128)}) custom-call(f32[128,512]{1,0:T(8,128)} %get-tuple-element.4.zscore_ref, f32[128,128]{1,0:T(8,128)} %get-tuple-element.5.thresholds_ref), custom_call_target="tpu_custom_call" | custom-call | tf_op jit(solution)/shard_map/pallas_call | solution.py:579

commit v4 on v3

--- a/solution.py
+++ b/solution.py
@@ -16,27 +16,27 @@
 MESH = pl.DeviceIdType.MESH
 
 order = [
-    ("gather", 0), ("gather", 1), ("gather", 2), ("own", 0, 0), ("gather", 3), ("gather", 4),
-    ("passed", 0, 0), ("gather", 5), ("own", 0, 1), ("gather", 6), ("ring", 0, 0), ("passed", 0, 1),
-    ("gather", 7), ("gather", 8), ("own", 1, 0), ("ring", 0, 2), ("gather", 9), ("ring", 0, 1),
-    ("passed", 1, 0), ("gather", 10), ("far", 0, 0), ("gather", 11), ("own", 1, 1), ("passed", 1, 1),
-    ("ring", 1, 0), ("side", 0, 0), ("ring", 0, 3), ("far", 0, 2), ("gather", 12), ("gather", 13),
-    ("ring", 1, 2), ("gather", 14), ("own", 2, 0), ("far", 0, 1), ("passed", 2, 0), ("gather", 15),
-    ("side", 0, 2), ("far", 1, 0), ("side", 0, 3), ("ring", 1, 3), ("gather", 16), ("ring", 1, 1),
-    ("far", 1, 2), ("gather", 17), ("own", 2, 1), ("side", 0, 1), ("far", 0, 3), ("side", 1, 0),
-    ("passed", 2, 1), ("gather", 18), ("ring", 2, 2), ("gather", 19), ("ring", 2, 0), ("gather", 20),
-    ("own", 3, 0), ("side", 1, 3), ("passed", 3, 0), ("corner", 0, 1), ("gather", 21), ("side", 1, 2),
-    ("far", 1, 1), ("corner", 0, 3), ("gather", 22), ("ring", 2, 1), ("side", 1, 1), ("corner", 0, 0),
-    ("corner", 1, 0), ("far", 1, 3), ("ring", 2, 3), ("corner", 0, 2), ("gather", 23), ("own", 3, 1),
-    ("corner", 1, 1), ("far", 2, 0), ("passed", 3, 1), ("ring", 3, 0), ("ring", 3, 2), ("far", 2, 1),
-    ("corner", 1, 3), ("far", 2, 3), ("ring", 3, 1), ("corner", 1, 2), ("end", 0, 0), ("far", 2, 2),
-    ("side", 2, 0), ("side", 2, 1), ("end", 0, 1), ("ring", 3, 3), ("corner", 2, 0), ("side", 2, 2),
-    ("multiply", 0, 0), ("multiply", 0, 1), ("side", 2, 3), ("end", 1, 0), ("end", 1, 1), ("far", 3, 2),
-    ("corner", 2, 2), ("far", 3, 1), ("corner", 2, 1), ("far", 3, 0), ("far", 3, 3), ("corner", 2, 3),
-    ("side", 3, 2), ("side", 3, 0), ("multiply", 1, 0), ("multiply", 1, 1), ("finish", 0), ("side", 3, 1),
-    ("side", 3, 3), ("corner", 3, 2), ("corner", 3, 0), ("end", 2, 0), ("multiply", 2, 0), ("corner", 3, 3),
-    ("corner", 3, 1), ("end", 2, 1), ("multiply", 2, 1), ("finish", 1), ("end", 3, 0), ("multiply", 3, 0),
-    ("end", 3, 1), ("multiply", 3, 1), ("finish", 2),
+    ("gather", 0), ("gather", 1), ("gather", 2), ("own", 0, 0), ("gather", 3), ("gather", 4), ("gather", 5),
+    ("own", 0, 1), ("gather", 6), ("gather", 7), ("passed", 0, 0), ("passed", 0, 1), ("gather", 8),
+    ("ring", 0, 0), ("own", 1, 0), ("gather", 9), ("passed", 1, 0), ("gather", 10), ("gather", 11),
+    ("own", 1, 1), ("ring", 0, 1), ("gather", 12), ("passed", 1, 1), ("ring", 0, 2), ("gather", 13),
+    ("ring", 0, 3), ("ring", 1, 0), ("gather", 14), ("own", 2, 0), ("side", 0, 0), ("ring", 1, 2),
+    ("passed", 2, 0), ("gather", 15), ("far", 0, 0), ("gather", 16), ("gather", 17), ("own", 2, 1),
+    ("passed", 2, 1), ("ring", 1, 1), ("far", 0, 1), ("side", 0, 1), ("far", 0, 2), ("gather", 18),
+    ("side", 0, 2), ("side", 0, 3), ("far", 1, 0), ("gather", 19), ("ring", 1, 3), ("ring", 2, 2),
+    ("gather", 20), ("own", 3, 0), ("gather", 21), ("ring", 2, 0), ("passed", 3, 0), ("gather", 22),
+    ("far", 0, 3), ("corner", 0, 1), ("corner", 0, 0), ("gather", 23), ("ring", 2, 3), ("own", 3, 1),
+    ("ring", 2, 1), ("far", 1, 1), ("passed", 3, 1), ("far", 1, 2), ("far", 1, 3), ("corner", 0, 2),
+    ("side", 1, 2), ("side", 1, 0), ("corner", 0, 3), ("ring", 3, 0), ("far", 2, 3), ("ring", 3, 2),
+    ("ring", 3, 1), ("far", 2, 1), ("ring", 3, 3), ("far", 2, 0), ("side", 1, 1), ("end", 0, 0),
+    ("side", 1, 3), ("far", 2, 2), ("multiply", 0, 0), ("corner", 1, 0), ("corner", 1, 2), ("far", 3, 0),
+    ("end", 0, 1), ("far", 3, 2), ("side", 2, 0), ("corner", 1, 1), ("multiply", 0, 1), ("corner", 1, 3),
+    ("side", 2, 2), ("far", 3, 1), ("corner", 2, 0), ("side", 2, 1), ("side", 3, 0), ("far", 3, 3),
+    ("side", 2, 3), ("corner", 2, 1), ("corner", 2, 3), ("corner", 2, 2), ("side", 3, 2), ("end", 1, 0),
+    ("multiply", 1, 0), ("side", 3, 3), ("corner", 3, 2), ("end", 1, 1), ("corner", 3, 0), ("side", 3, 1),
+    ("multiply", 1, 1), ("corner", 3, 1), ("corner", 3, 3), ("end", 2, 0), ("multiply", 2, 0), ("end", 2, 1),
+    ("multiply", 2, 1), ("finish", 0), ("end", 3, 0), ("multiply", 3, 0), ("end", 3, 1), ("multiply", 3, 1),
+    ("finish", 1), ("finish", 2),
 ]
 straight_ring = ()
 straight_side = ()
@@ -72,7 +72,7 @@
 
 def kernel(
     dosage_ref, pheno_ref, index_ref, seg_ref, zscore_ref, thresholds_ref,
-    traits, words, table, index, counts, dose, permuted, score, arrived, stats, marks,
+    traits, words, table, index, counts, dose, permuted, score, row_sum, leaving, arrived, stats, marks,
     best, best_x, best_xy, best_y,
     local_sem, trait_send, trait_recv, stat_send, stat_recv, dose_send, dose_recv,
     pass_send, pass_recv, perm_send, perm_recv, score_send, score_recv,
@@ -186,6 +186,8 @@
     )
     for r in range(high):
         table[pl.ds(8 * r, 8), :] = jnp.broadcast_to(words[pl.ds(r, 1), :], (8, 128))
+    held = (fixed.astype(jnp.float32) * unit).astype(jnp.bfloat16).astype(jnp.float32)
+    held_sum = jnp.sum(jnp.sum(held, axis=0, keepdims=True), axis=1, keepdims=True)
     scale = jnp.broadcast_to(unit, (8, 128))
     read_index.wait()
 
@@ -319,17 +321,29 @@
             product = jnp.dot(
                 left, dose[pl.ds(aligned(q * part, 16), part), :], preferred_element_type=jnp.float32
             )
+            tiles = [left[:, 128 * t : 128 * (t + 1)].astype(jnp.float32) for t in range(part // 128)]
+            while len(tiles) > 1:
+                tiles = [sum(tiles[t : t + 2]) for t in range(0, len(tiles), 2)]
             if half:
                 score[k] += product
+                row_sum[...] += tiles[0]
             else:
 
                 @pl.when(i == 0)
                 def _():
                     score[k] = product
+                    row_sum[...] = tiles[0]
 
                 @pl.when(i > 0)
                 def _():
                     score[k] += product
+                    row_sum[...] += tiles[0]
+
+    def center(k, mean_dose):
+        sums = jnp.sum(row_sum[...], axis=1, keepdims=True)
+        value = score[k] - sums * mean_dose
+        score[k] = value
+        leaving[k] = value.astype(jnp.bfloat16)
 
     def score_copies(k):
         copies = []
@@ -337,7 +351,7 @@
             to = lax.rem(z + d, side)
             copies.append(
                 remote(
-                    score.at[k, pl.ds(aligned(to * 2 * rows, 2 * rows), 2 * rows)],
+                    leaving.at[k, pl.ds(aligned(to * 2 * rows, 2 * rows), 2 * rows)],
                     arrived.at[k, d - 1], score_send.at[k, d - 1], score_recv.at[k, d - 1],
                     to_samp=to * 2 + core,
                 )
@@ -350,7 +364,8 @@
         sums = jnp.sum(stats[...], axis=0)
         allele_sum, allele_sq = sums[0:1], sums[1:2]
         allele_var = allele_sq / all_samples - (allele_sum / all_samples) ** 2
-        return 1.0 / jnp.sqrt(all_samples * (pheno_var + epsilon) * (allele_var + epsilon))
+        inverse = 1.0 / jnp.sqrt(all_samples * (pheno_var + epsilon) * (allele_var + epsilon))
+        return inverse, allele_sum / all_samples
 
     lane = lax.broadcasted_iota(jnp.int32, (2 * rows, 128), 1)
 
@@ -363,13 +378,13 @@
             offset *= 2
         return ends - 1 - var * width
 
-    def finish(k, inverse, ends):
+    def finish(k, inverse, shared, ends):
         for copy in score_copies(k):
             copy.wait_recv()
         total = score[k, pl.ds(aligned(z * 2 * rows, 2 * rows), 2 * rows), :]
         for d in range(3):
-            total = total + arrived[k, d]
-        result = total * inverse
+            total = total + arrived[k, d].astype(jnp.float32)
+        result = (total + shared) * inverse
         zscore_ref[pl.ds(rows * k, rows), :] = result[:rows]
         zscore_ref[pl.ds(64 + rows * k, rows), :] = result[rows:]
         size = jnp.abs(result)
@@ -394,7 +409,7 @@
                 axis=0,
             )
             best_here = jnp.maximum(best_here, found)
-        best[k] = best_here
+        best[k] = best_here.astype(jnp.bfloat16)
 
     def best_copies(k, axis):
         source, target = (best, best_x) if axis == 0 else (best_xy, best_y)
@@ -418,6 +433,7 @@
         value = best_xy[k]
         for d in range(3):
             value = jnp.maximum(value, best_y[k, d])
+        value = value.astype(jnp.float32)
         thresholds_ref[pl.ds(rows * k, rows), :] = value[:rows]
         thresholds_ref[pl.ds(64 + rows * k, rows), :] = value[rows:]
 
@@ -460,12 +476,14 @@
             k, half = where
             if k == 0 and half == 0:
                 wait_dose()
-                inverse = inverse_divisor()
+                inverse, mean_dose = inverse_divisor()
+                shared = held_sum * mean_dose
             multiply(k, half)
             if half:
+                center(k, mean_dose)
                 start(score_copies(k))
         elif name == "finish":
-            finish(*where, inverse, ends)
+            finish(*where, inverse, shared, ends)
             finished.extend(where)
         else:
             stage(*where, name, go)
@@ -477,7 +495,7 @@
     for k in range(last - 1):
         join_x(k)
         start(best_copies(k, 1))
-    finish(last, inverse, ends)
+    finish(last, inverse, shared, ends)
     start(best_copies(last, 0))
     join_x(last - 1)
     start(best_copies(last - 1, 1))
@@ -542,13 +560,15 @@
             vmem((2 * samples, width), bf16),
             vmem((chunks, 9, rows, 2 * samples), bf16),
             vmem((chunks, 8 * rows, width), f32),
-            vmem((chunks, 3, 2 * rows, width), f32),
+            vmem((8 * rows, 128), f32),
+            vmem((chunks, 8 * rows, width), bf16),
+            vmem((chunks, 3, 2 * rows, width), bf16),
             vmem((8, 8, width), f32),
             vmem((1, segments), i32),
-            vmem((chunks, 2 * rows, segments), f32),
-            vmem((chunks, 3, 2 * rows, segments), f32),
-            vmem((chunks, 2 * rows, segments), f32),
-            vmem((chunks, 3, 2 * rows, segments), f32),
+            vmem((chunks, 2 * rows, segments), bf16),
+            vmem((chunks, 3, 2 * rows, segments), bf16),
+            vmem((chunks, 2 * rows, segments), bf16),
+            vmem((chunks, 3, 2 * rows, segments), bf16),
             dma((3 + pieces,)),
             dma((7,)),
             dma((7,)),

time: 83.8 us -> 79.8 us (0.952)
  Pallas kernels: 82.8 us -> 78.7 us
    pallas_call x1, Pallas kernels: 81.1 us -> 77 us  [per_device(): pl.pallas_call(kernel, out_shape=outs, in_specs=[any_space] * 4, out_spec...]
where the time goes in v4:
time: 79.8 us; the launch traced here: 79.5 us
  Pallas kernels  78.7 us (99%)
  between operations  0.8 us (1%)
    pallas_call x1, Pallas kernels, per_device(): pl.pallas_call(kernel, out_shape=outs, in_specs=[any_space] * 4, out_spec...  77 us
    pallas_call x1, Pallas kernels, per_device(): pl.pallas_call(keep_kernel, out_shape=outs, in_specs=[any_space] * 2, out...  1.7 us

profile of v4, /device:TPU:0, one launch (start us, length us, event | category | flops | bytes accessed | tf_op | source)
XLA Modules:
  0.0 79.5 jit_solution(9421945345772346136)
XLA Ops:
  0.6 77.0 %shard_map.59 = (f32[128,512]{1,0:T(8,128)}, f32[128,128]{1,0:T(8,128)}) custom-call(s32[3072,512]{1,0:T(8,128)} %dosage_ref.1, f32[24,128]{1,0:T(8,128)} %bitcast.2, s32[64,3072]{1,0:T(8,128)} %index_ref.1, s32[1,128]{1,0:T(1,128)} %bitcast.3), custom_call_target="tpu_custom_call" | custom-call | tf_op jit(solution)/shard_map/pallas_call | solution.py:549
  77.6 1.7 %shard_map.60 = (f32[128,512]{1,0:T(8,128)}, f32[128,128]{1,0:T(8,128)}) custom-call(f32[128,512]{1,0:T(8,128)} %get-tuple-element.4.zscore_ref, f32[128,128]{1,0:T(8,128)} %get-tuple-element.5.thresholds_ref), custom_call_target="tpu_custom_call" | custom-call | tf_op jit(solution)/shard_map/pallas_call | solution.py:599

commit v5 on v4

--- a/solution.py
+++ b/solution.py
@@ -17,29 +17,27 @@
 
 order = [
     ("gather", 0), ("gather", 1), ("gather", 2), ("own", 0, 0), ("gather", 3), ("gather", 4), ("gather", 5),
-    ("own", 0, 1), ("gather", 6), ("gather", 7), ("passed", 0, 0), ("passed", 0, 1), ("gather", 8),
-    ("ring", 0, 0), ("own", 1, 0), ("gather", 9), ("passed", 1, 0), ("gather", 10), ("gather", 11),
-    ("own", 1, 1), ("ring", 0, 1), ("gather", 12), ("passed", 1, 1), ("ring", 0, 2), ("gather", 13),
-    ("ring", 0, 3), ("ring", 1, 0), ("gather", 14), ("own", 2, 0), ("side", 0, 0), ("ring", 1, 2),
-    ("passed", 2, 0), ("gather", 15), ("far", 0, 0), ("gather", 16), ("gather", 17), ("own", 2, 1),
-    ("passed", 2, 1), ("ring", 1, 1), ("far", 0, 1), ("side", 0, 1), ("far", 0, 2), ("gather", 18),
-    ("side", 0, 2), ("side", 0, 3), ("far", 1, 0), ("gather", 19), ("ring", 1, 3), ("ring", 2, 2),
-    ("gather", 20), ("own", 3, 0), ("gather", 21), ("ring", 2, 0), ("passed", 3, 0), ("gather", 22),
-    ("far", 0, 3), ("corner", 0, 1), ("corner", 0, 0), ("gather", 23), ("ring", 2, 3), ("own", 3, 1),
-    ("ring", 2, 1), ("far", 1, 1), ("passed", 3, 1), ("far", 1, 2), ("far", 1, 3), ("corner", 0, 2),
-    ("side", 1, 2), ("side", 1, 0), ("corner", 0, 3), ("ring", 3, 0), ("far", 2, 3), ("ring", 3, 2),
-    ("ring", 3, 1), ("far", 2, 1), ("ring", 3, 3), ("far", 2, 0), ("side", 1, 1), ("end", 0, 0),
-    ("side", 1, 3), ("far", 2, 2), ("multiply", 0, 0), ("corner", 1, 0), ("corner", 1, 2), ("far", 3, 0),
-    ("end", 0, 1), ("far", 3, 2), ("side", 2, 0), ("corner", 1, 1), ("multiply", 0, 1), ("corner", 1, 3),
-    ("side", 2, 2), ("far", 3, 1), ("corner", 2, 0), ("side", 2, 1), ("side", 3, 0), ("far", 3, 3),
-    ("side", 2, 3), ("corner", 2, 1), ("corner", 2, 3), ("corner", 2, 2), ("side", 3, 2), ("end", 1, 0),
-    ("multiply", 1, 0), ("side", 3, 3), ("corner", 3, 2), ("end", 1, 1), ("corner", 3, 0), ("side", 3, 1),
-    ("multiply", 1, 1), ("corner", 3, 1), ("corner", 3, 3), ("end", 2, 0), ("multiply", 2, 0), ("end", 2, 1),
-    ("multiply", 2, 1), ("finish", 0), ("end", 3, 0), ("multiply", 3, 0), ("end", 3, 1), ("multiply", 3, 1),
-    ("finish", 1), ("finish", 2),
+    ("own", 0, 1), ("passed", 0, 0), ("gather", 6), ("gather", 7), ("passed", 0, 1), ("ring", 0, 0),
+    ("gather", 8), ("own", 1, 0), ("gather", 9), ("passed", 1, 0), ("gather", 10), ("ring", 0, 2),
+    ("gather", 11), ("ring", 0, 1), ("own", 1, 1), ("passed", 1, 1), ("ring", 0, 3), ("gather", 12),
+    ("ring", 1, 0), ("gather", 13), ("ring", 1, 2), ("gather", 14), ("far", 0, 0), ("side", 0, 0),
+    ("own", 2, 0), ("gather", 15), ("far", 0, 1), ("passed", 2, 0), ("far", 0, 2), ("side", 0, 2),
+    ("gather", 16), ("ring", 1, 3), ("far", 0, 3), ("gather", 17), ("own", 2, 1), ("ring", 1, 1),
+    ("far", 1, 0), ("gather", 18), ("passed", 2, 1), ("side", 0, 1), ("ring", 2, 0), ("side", 0, 3),
+    ("gather", 19), ("far", 1, 2), ("ring", 2, 2), ("gather", 20), ("corner", 0, 1), ("own", 3, 0),
+    ("corner", 0, 3), ("gather", 21), ("side", 1, 2), ("side", 1, 0), ("passed", 3, 0), ("gather", 22),
+    ("far", 1, 1), ("ring", 2, 1), ("gather", 23), ("own", 3, 1), ("corner", 0, 0), ("far", 1, 3),
+    ("ring", 2, 3), ("passed", 3, 1), ("far", 2, 0), ("end", 0, 1), ("side", 1, 1), ("side", 1, 3),
+    ("corner", 0, 2), ("corner", 1, 1), ("far", 2, 1), ("corner", 1, 0), ("far", 2, 2), ("far", 2, 3),
+    ("ring", 3, 0), ("corner", 1, 2), ("ring", 3, 2), ("corner", 1, 3), ("ring", 3, 1), ("ring", 3, 3),
+    ("side", 2, 0), ("side", 2, 2), ("side", 2, 3), ("corner", 2, 2), ("corner", 2, 0), ("end", 0, 0),
+    ("multiply", 0, 0), ("side", 2, 1), ("multiply", 0, 1), ("far", 3, 0), ("far", 3, 1), ("far", 3, 2),
+    ("side", 3, 0), ("corner", 2, 1), ("far", 3, 3), ("end", 1, 1), ("corner", 2, 3), ("end", 1, 0),
+    ("side", 3, 2), ("multiply", 1, 0), ("multiply", 1, 1), ("side", 3, 1), ("end", 2, 0), ("corner", 3, 2),
+    ("corner", 3, 0), ("side", 3, 3), ("multiply", 2, 0), ("corner", 3, 1), ("corner", 3, 3), ("end", 2, 1),
+    ("multiply", 2, 1), ("finish", 0), ("finish", 1), ("end", 3, 0), ("multiply", 3, 0), ("end", 3, 1),
+    ("multiply", 3, 1), ("finish", 2),
 ]
-straight_ring = ()
-straight_side = ()
 
 
 def looked_up(index, table_ref, half_at):
@@ -71,10 +69,10 @@
 
 
 def kernel(
-    dosage_ref, pheno_ref, index_ref, seg_ref, zscore_ref, thresholds_ref,
+    dosage_ref, pheno_ref, index_ref, seg_ref, zscore_out, thresholds_out, zscore_ref, thresholds_ref,
     traits, words, table, index, counts, dose, permuted, score, row_sum, leaving, arrived, stats, marks,
     best, best_x, best_xy, best_y,
-    local_sem, trait_send, trait_recv, stat_send, stat_recv, dose_send, dose_recv,
+    local_sem, trait_send, trait_recv, stat_recv, dose_send, dose_recv,
     pass_send, pass_recv, perm_send, perm_recv, score_send, score_recv,
     x_send, x_recv, y_send, y_recv,
 ):
@@ -132,9 +130,9 @@
         for d in range(7)
     ]
 
-    def dose_copy(i):
-        at_rows = pl.ds(aligned(core * samples + i * piece, 16), piece)
-        return remote(dose.at[at_rows], dose.at[at_rows], dose_send.at[i], dose_recv.at[i], to_samp=samp ^ 1)
+    def dose_copy(of_core):
+        at_rows = pl.ds(aligned(of_core * samples, 16), samples)
+        return remote(dose.at[at_rows], dose.at[at_rows], dose_send.at[0], dose_recv.at[0], to_samp=samp ^ 1)
 
     def convert(i):
         read_dose[i].wait()
@@ -158,7 +156,7 @@
         stats[samp, 1:2, :] += jnp.sum(two, axis=0, keepdims=True)
 
     stat_copies = [
-        remote(stats.at[samp], stats.at[samp], stat_send.at[d], stat_recv.at[d], to_samp=samp_peers[d])
+        remote(stats.at[samp], stats.at[samp], trait_send.at[d], stat_recv.at[d], to_samp=samp_peers[d])
         for d in range(7)
     ]
 
@@ -213,12 +211,14 @@
         q = 2 * from_core + half
         return remote(
             permuted.at[k, 8, :, lanes(q)], permuted.at[k, own_slot, :, lanes(q)],
-            pass_send.at[k, half], pass_recv.at[k, half], to_samp=samp ^ 1,
+            pass_send.at[half], pass_recv.at[k, half], to_samp=samp ^ 1,
         )
 
     def pass_on(k, half):
         @pl.when(jnp.logical_not(is_source))
         def _():
+            if k:
+                passed(k - 1, half, core).wait_send()
             passed(k, half, core).start()
 
     def moved(axis, by):
@@ -228,7 +228,7 @@
         return [
             remote(
                 permuted.at[k, slot, :, lanes(q)], permuted.at[k, slot, :, lanes(q)],
-                perm_send.at[k, q, event + i], perm_recv.at[k, q, slot], to_var=moved(axis, by),
+                perm_send.at[q, event + i], perm_recv.at[k, q, slot], to_var=moved(axis, by),
             )
             for i, (axis, by) in enumerate(directions)
         ]
@@ -236,7 +236,7 @@
     def recv(k, q, slot):
         remote(
             permuted.at[k, slot, :, lanes(q)], permuted.at[k, slot, :, lanes(q)],
-            perm_send.at[k, q, 0], perm_recv.at[k, q, slot],
+            perm_send.at[q, 0], perm_recv.at[k, q, slot],
         ).wait_recv()
 
     def slot_of(dx, dy):
@@ -246,35 +246,27 @@
     def routes(q):
         return q % 2, (1 if q < 2 else -1)
 
-    def cells(k, q, level):
+    def cells(q, level):
         axis, way = routes(q)
         other = 1 - axis
-        unit_no = 2 * k + q % 2
-        straight = unit_no in straight_ring
         both = [(other, way), (other, -way)]
-        if unit_no in straight_side:
-            both.append((other, 2 * way))
         near, back = way % side, -way % side
         if level == "own":
-            ring = [(axis, way), (axis, -way)] + [(axis, 2 * way)] * straight
-            found = [(0, 0, 0, ring + both)]
+            found = [(0, 0, 0, [(axis, way), (axis, -way), *both])]
         elif level == "ring":
-            found = [(near, 0, 6, [(axis, way)] * (not straight) + both), (back, 0, 10, both)]
+            found = [(near, 0, 4, [(axis, way), *both]), (back, 0, 7, both)]
         elif level == "far":
-            found = [(2, 0, 13, both)]
-        elif unit_no in straight_side:
-            ends = level == "end"
-            found = [(d, s, 0, []) for s in (near, back, 2) for d in range(side) if ends]
+            found = [(2, 0, 9, both)]
         elif level == "side":
-            found = [(d, near, 16 + i, [(other, way)]) for i, d in enumerate((0, near, back))]
+            found = [(d, near, 11 + i, [(other, way)]) for i, d in enumerate((0, near, back))]
         elif level == "corner":
-            found = [(2, near, 19, [(other, way)])]
+            found = [(2, near, 14, [(other, way)])]
         else:
             found = [(d, s, 0, []) for s in (back, 2) for d in range(side)]
         return [(p, s, *rest) if axis == 0 else (s, p, *rest) for p, s, *rest in found]
 
     def stage(k, q, level, act):
-        todo = cells(k, q, level)
+        todo = cells(q, level)
         for dy in dict.fromkeys(t[1] for t in todo):
 
             @pl.when(slot_of(0, dy)[1])
@@ -286,12 +278,21 @@
     def go(k, q, level, slot, event, ways):
         if level != "own":
             recv(k, q, slot)
+        earlier = before.get((q, level)) if level != "own" else (k - 1 if k else None)
+        if ways and earlier is not None:
+            done(earlier, q, level, slot, event, ways)
         for copy in sends(k, q, event, slot, ways):
             copy.start()
 
     def done(k, q, level, slot, event, ways):
         for copy in sends(k, q, event, slot, ways):
             copy.wait_send()
+
+    before = {}
+
+    def step(k, q, level):
+        stage(k, q, level, go)
+        before[q, level] = k
 
     def send_own(k, half):
         for q in range(parts):
@@ -352,7 +353,7 @@
             copies.append(
                 remote(
                     leaving.at[k, pl.ds(aligned(to * 2 * rows, 2 * rows), 2 * rows)],
-                    arrived.at[k, d - 1], score_send.at[k, d - 1], score_recv.at[k, d - 1],
+                    arrived.at[k, d - 1], score_send.at[d - 1], score_recv.at[k, d - 1],
                     to_samp=to * 2 + core,
                 )
             )
@@ -415,7 +416,7 @@
         source, target = (best, best_x) if axis == 0 else (best_xy, best_y)
         send, recv_sem = (x_send, x_recv) if axis == 0 else (y_send, y_recv)
         return [
-            remote(source.at[k], target.at[k, d - 1], send.at[k, d - 1], recv_sem.at[k, d - 1], to_var=moved(axis, d))
+            remote(source.at[k], target.at[k, d - 1], send.at[d - 1], recv_sem.at[k, d - 1], to_var=moved(axis, d))
             for d in (1, 3, 2)
         ]
 
@@ -437,14 +438,21 @@
         thresholds_ref[pl.ds(rows * k, rows), :] = value[:rows]
         thresholds_ref[pl.ds(64 + rows * k, rows), :] = value[rows:]
 
+    def sent_all(copies):
+        for copy in copies:
+            copy.wait_send()
+
+    def send_best(k, axis):
+        if k:
+            sent_all(best_copies(k - 1, axis))
+        start(best_copies(k, axis))
+
     def start(copies):
         for copy in copies:
             copy.start()
 
     def wait_dose():
-        for i in range(pieces):
-            theirs = pl.ds(aligned((1 - core) * samples + i * piece, 16), piece)
-            remote(dose.at[theirs], dose.at[theirs], dose_send.at[i], dose_recv.at[i]).wait_recv()
+        dose_copy(1 - core).wait_recv()
 
     def drain_passed(k):
         @pl.when(jnp.logical_not(is_source))
@@ -459,7 +467,8 @@
         if name == "gather":
             gather(*where)
             if where[0] == 0:
-                start([dose_copy(i) for i in range(pieces)] + stat_copies)
+                sent_all(trait_copies)
+                start([dose_copy(core)] + stat_copies)
             if where[0] == 3:
                 read_seg.wait()
                 ends = local_ends()
@@ -481,40 +490,47 @@
             multiply(k, half)
             if half:
                 center(k, mean_dose)
+                if k:
+                    sent_all(score_copies(k - 1))
                 start(score_copies(k))
         elif name == "finish":
             finish(*where, inverse, shared, ends)
             finished.extend(where)
         else:
-            stage(*where, name, go)
+            step(*where, name)
         if (name, *where) == last_send:
             sent = True
         while sent and len(started) < len(finished):
             started.append(finished[len(started)])
-            start(best_copies(started[-1], 0))
+            send_best(started[-1], 0)
     for k in range(last - 1):
         join_x(k)
-        start(best_copies(k, 1))
+        send_best(k, 1)
     finish(last, inverse, shared, ends)
-    start(best_copies(last, 0))
+    keep_zscore = pltpu.make_async_copy(zscore_ref, zscore_out, local_sem.at[0])
+    keep_zscore.start()
+    send_best(last, 0)
     join_x(last - 1)
-    start(best_copies(last - 1, 1))
-    for copy in trait_copies + stat_copies + [dose_copy(i) for i in range(pieces)]:
-        copy.wait_send()
-    for k in range(chunks):
-        drain_passed(k)
-        for q in range(parts):
-            for level in ("own", "ring", "far", "side", "corner"):
-                stage(k, q, level, done)
-        for copy in score_copies(k):
-            copy.wait_send()
+    send_best(last - 1, 1)
+    sent_all(stat_copies + [dose_copy(core)])
+    drain_passed(last)
+    for q in range(parts):
+        stage(last, q, "own", done)
+        for level in ("ring", "far", "side", "corner"):
+            stage(before[q, level], q, level, done)
+    sent_all(score_copies(last))
+    for k in range(last - 1):
+        join_y(k)
     join_x(last)
-    start(best_copies(last, 1))
-    for k in range(chunks):
-        join_y(k)
-    for k in range(chunks):
-        for copy in best_copies(k, 0) + best_copies(k, 1):
-            copy.wait_send()
+    send_best(last, 1)
+    join_y(last - 1)
+    sent_all(best_copies(last, 0))
+    join_y(last)
+    keep = pltpu.make_async_copy(thresholds_ref, thresholds_out, local_sem.at[1])
+    keep.start()
+    sent_all(best_copies(last, 1))
+    keep_zscore.wait()
+    keep.wait()
 
 
 def keep_kernel(zscore_ref, thresholds_ref, zscore_out, thresholds_out, first, second, sem):
@@ -550,8 +566,10 @@
         kernel,
         out_shape=outs,
         in_specs=[any_space] * 4,
-        out_specs=(pl.BlockSpec(memory_space=vmem), pl.BlockSpec(memory_space=vmem)),
+        out_specs=(any_space, any_space),
         scratch_shapes=[
+            vmem((128, width), f32),
+            vmem((128, segments), f32),
             vmem((8, samples // 128, 128), f32),
             vmem((samples * 4 // 128, 128), i32),
             vmem((samples * 4 // 16, 128), i32),
@@ -573,18 +591,17 @@
             dma((7,)),
             dma((7,)),
             dma((7,)),
-            dma((7,)),
-            dma((pieces,)),
-            dma((pieces,)),
+            dma((1,)),
+            dma((1,)),
+            dma((2,)),
             dma((chunks, 2)),
-            dma((chunks, 2)),
-            dma((chunks, parts, 20)),
+            dma((parts, 15)),
             dma((chunks, parts, 8)),
+            dma((3,)),
             dma((chunks, 3)),
+            dma((3,)),
             dma((chunks, 3)),
-            dma((chunks, 3)),
-            dma((chunks, 3)),
-            dma((chunks, 3)),
+            dma((3,)),
             dma((chunks, 3)),
         ],
         compiler_params=pltpu.CompilerParams(

time: 79.8 us -> 76.4 us (0.957)
  Pallas kernels: 78.7 us -> 75.5 us
    pallas_call x1, Pallas kernels: 77 us -> 73.8 us  [per_device(): pl.pallas_call(kernel, out_shape=outs, in_specs=[any_space] * 4, out_spec...]
where the time goes in v5:
time: 76.4 us; the launch traced here: 76.3 us
  Pallas kernels  75.5 us (99%)
  between operations  0.8 us (1%)
    pallas_call x1, Pallas kernels, per_device(): pl.pallas_call(kernel, out_shape=outs, in_specs=[any_space] * 4, out_spec...  73.8 us
    pallas_call x1, Pallas kernels, per_device(): pl.pallas_call(keep_kernel, out_shape=outs, in_specs=[any_space] * 2, out...  1.7 us

profile of v5, /device:TPU:0, one launch (start us, length us, event | category | flops | bytes accessed | tf_op | source)
XLA Modules:
  0.0 76.3 jit_solution(15621606019352512774)
XLA Ops:
  0.6 73.8 %shard_map.59 = (f32[128,512]{1,0:T(8,128)}, f32[128,128]{1,0:T(8,128)}) custom-call(s32[3072,512]{1,0:T(8,128)} %dosage_ref.1, f32[24,128]{1,0:T(8,128)} %bitcast.2, s32[64,3072]{1,0:T(8,128)} %index_ref.1, s32[1,128]{1,0:T(1,128)} %bitcast.3), custom_call_target="tpu_custom_call" | custom-call | tf_op jit(solution)/shard_map/pallas_call | solution.py:565
  74.4 1.7 %shard_map.60 = (f32[128,512]{1,0:T(8,128)}, f32[128,128]{1,0:T(8,128)}) custom-call(f32[128,512]{1,0:T(8,128)} %get-tuple-element.4.zscore_ref, f32[128,128]{1,0:T(8,128)} %get-tuple-element.5.thresholds_ref), custom_call_target="tpu_custom_call" | custom-call | tf_op jit(solution)/shard_map/pallas_call | solution.py:616

commit v6 on v5

--- a/solution.py
+++ b/solution.py
@@ -16,27 +16,27 @@
 MESH = pl.DeviceIdType.MESH
 
 order = [
-    ("gather", 0), ("gather", 1), ("gather", 2), ("own", 0, 0), ("gather", 3), ("gather", 4), ("gather", 5),
-    ("own", 0, 1), ("passed", 0, 0), ("gather", 6), ("gather", 7), ("passed", 0, 1), ("ring", 0, 0),
-    ("gather", 8), ("own", 1, 0), ("gather", 9), ("passed", 1, 0), ("gather", 10), ("ring", 0, 2),
-    ("gather", 11), ("ring", 0, 1), ("own", 1, 1), ("passed", 1, 1), ("ring", 0, 3), ("gather", 12),
-    ("ring", 1, 0), ("gather", 13), ("ring", 1, 2), ("gather", 14), ("far", 0, 0), ("side", 0, 0),
-    ("own", 2, 0), ("gather", 15), ("far", 0, 1), ("passed", 2, 0), ("far", 0, 2), ("side", 0, 2),
-    ("gather", 16), ("ring", 1, 3), ("far", 0, 3), ("gather", 17), ("own", 2, 1), ("ring", 1, 1),
-    ("far", 1, 0), ("gather", 18), ("passed", 2, 1), ("side", 0, 1), ("ring", 2, 0), ("side", 0, 3),
-    ("gather", 19), ("far", 1, 2), ("ring", 2, 2), ("gather", 20), ("corner", 0, 1), ("own", 3, 0),
-    ("corner", 0, 3), ("gather", 21), ("side", 1, 2), ("side", 1, 0), ("passed", 3, 0), ("gather", 22),
-    ("far", 1, 1), ("ring", 2, 1), ("gather", 23), ("own", 3, 1), ("corner", 0, 0), ("far", 1, 3),
-    ("ring", 2, 3), ("passed", 3, 1), ("far", 2, 0), ("end", 0, 1), ("side", 1, 1), ("side", 1, 3),
-    ("corner", 0, 2), ("corner", 1, 1), ("far", 2, 1), ("corner", 1, 0), ("far", 2, 2), ("far", 2, 3),
-    ("ring", 3, 0), ("corner", 1, 2), ("ring", 3, 2), ("corner", 1, 3), ("ring", 3, 1), ("ring", 3, 3),
-    ("side", 2, 0), ("side", 2, 2), ("side", 2, 3), ("corner", 2, 2), ("corner", 2, 0), ("end", 0, 0),
-    ("multiply", 0, 0), ("side", 2, 1), ("multiply", 0, 1), ("far", 3, 0), ("far", 3, 1), ("far", 3, 2),
-    ("side", 3, 0), ("corner", 2, 1), ("far", 3, 3), ("end", 1, 1), ("corner", 2, 3), ("end", 1, 0),
-    ("side", 3, 2), ("multiply", 1, 0), ("multiply", 1, 1), ("side", 3, 1), ("end", 2, 0), ("corner", 3, 2),
-    ("corner", 3, 0), ("side", 3, 3), ("multiply", 2, 0), ("corner", 3, 1), ("corner", 3, 3), ("end", 2, 1),
-    ("multiply", 2, 1), ("finish", 0), ("finish", 1), ("end", 3, 0), ("multiply", 3, 0), ("end", 3, 1),
-    ("multiply", 3, 1), ("finish", 2),
+    ("gather", 0), ("gather", 1), ("gather", 2), ("own", 0, 0), ("gather", 3), ("gather", 4),
+    ("passed", 0, 0), ("gather", 5), ("own", 0, 1), ("gather", 6), ("gather", 7), ("ring", 0, 0),
+    ("passed", 0, 1), ("gather", 8), ("own", 1, 0), ("gather", 9), ("passed", 1, 0), ("ring", 0, 2),
+    ("gather", 10), ("ring", 0, 1), ("gather", 11), ("own", 1, 1), ("far", 0, 0), ("gather", 12),
+    ("passed", 1, 1), ("ring", 1, 0), ("gather", 13), ("ring", 0, 3), ("ring", 1, 2), ("side", 0, 0),
+    ("far", 0, 2), ("gather", 14), ("own", 2, 0), ("gather", 15), ("side", 0, 1), ("side", 0, 2),
+    ("passed", 2, 0), ("gather", 16), ("far", 0, 1), ("gather", 17), ("own", 2, 1), ("passed", 2, 1),
+    ("ring", 1, 1), ("side", 0, 3), ("gather", 18), ("ring", 1, 3), ("ring", 2, 0), ("far", 1, 2),
+    ("far", 1, 0), ("gather", 19), ("far", 0, 3), ("gather", 20), ("own", 3, 0), ("corner", 0, 0),
+    ("ring", 2, 2), ("corner", 0, 2), ("passed", 3, 0), ("gather", 21), ("corner", 0, 1), ("gather", 22),
+    ("ring", 2, 1), ("ring", 2, 3), ("gather", 23), ("own", 3, 1), ("far", 1, 1), ("passed", 3, 1),
+    ("far", 1, 3), ("end", 0, 0), ("corner", 0, 3), ("far", 2, 0), ("far", 2, 1), ("ring", 3, 0),
+    ("side", 1, 1), ("side", 1, 2), ("side", 1, 0), ("ring", 3, 2), ("far", 2, 3), ("multiply", 0, 0),
+    ("ring", 3, 1), ("side", 1, 3), ("ring", 3, 3), ("corner", 1, 0), ("far", 2, 2), ("corner", 1, 3),
+    ("corner", 1, 2), ("far", 3, 0), ("end", 0, 1), ("corner", 1, 1), ("side", 2, 0), ("corner", 2, 0),
+    ("far", 3, 2), ("side", 2, 1), ("multiply", 0, 1), ("side", 2, 2), ("far", 3, 3), ("side", 2, 3),
+    ("corner", 2, 3), ("far", 3, 1), ("corner", 2, 1), ("side", 3, 0), ("corner", 2, 2), ("side", 3, 2),
+    ("end", 1, 0), ("multiply", 1, 0), ("corner", 3, 0), ("end", 1, 1), ("corner", 3, 2), ("side", 3, 3),
+    ("multiply", 1, 1), ("side", 3, 1), ("end", 2, 0), ("corner", 3, 1), ("corner", 3, 3), ("multiply", 2, 0),
+    ("end", 2, 1), ("multiply", 2, 1), ("finish", 0), ("end", 3, 0), ("multiply", 3, 0), ("finish", 1),
+    ("end", 3, 1), ("multiply", 3, 1), ("finish", 2),
 ]
 
 

time: 76.4 us -> 77.7 us (1.017)
  Pallas kernels: 75.5 us -> 76.8 us
    pallas_call x1, Pallas kernels: 73.8 us -> 75.1 us  [per_device(): pl.pallas_call(kernel, out_shape=outs, in_specs=[any_space] * 4, out_spec...]
where the time goes in v6:
time: 77.7 us; the launch traced here: 77.6 us
  Pallas kernels  76.8 us (99%)
  between operations  0.8 us (1%)
    pallas_call x1, Pallas kernels, per_device(): pl.pallas_call(kernel, out_shape=outs, in_specs=[any_space] * 4, out_spec...  75.1 us
    pallas_call x1, Pallas kernels, per_device(): pl.pallas_call(keep_kernel, out_shape=outs, in_specs=[any_space] * 2, out...  1.7 us

profile of v6, /device:TPU:0, one launch (start us, length us, event | category | flops | bytes accessed | tf_op | source)
XLA Modules:
  0.0 77.6 jit_solution(17377393453274532783)
XLA Ops:
  0.6 75.1 %shard_map.59 = (f32[128,512]{1,0:T(8,128)}, f32[128,128]{1,0:T(8,128)}) custom-call(s32[3072,512]{1,0:T(8,128)} %dosage_ref.1, f32[24,128]{1,0:T(8,128)} %bitcast.2, s32[64,3072]{1,0:T(8,128)} %index_ref.1, s32[1,128]{1,0:T(1,128)} %bitcast.3), custom_call_target="tpu_custom_call" | custom-call | tf_op jit(solution)/shard_map/pallas_call | solution.py:565
  75.7 1.7 %shard_map.60 = (f32[128,512]{1,0:T(8,128)}, f32[128,128]{1,0:T(8,128)}) custom-call(f32[128,512]{1,0:T(8,128)} %get-tuple-element.4.zscore_ref, f32[128,128]{1,0:T(8,128)} %get-tuple-element.5.thresholds_ref), custom_call_target="tpu_custom_call" | custom-call | tf_op jit(solution)/shard_map/pallas_call | solution.py:616
